TPU v7x, 64 devices: a 2x2x8 block of a 4x4x8 slice. The times are simulated.
64 devices in a mesh: data: 4 (over x, y), tensor: 16 (over z, core).
Axes of the slice: x: 2, y: 2, z: 8, core: 2. Of those that a mesh axis runs over, the one named last changes fastest.
The devices are a block of a 4x4x8 slice.
Arguments:
- x: bfloat16 [128, 32, 2560], P('data'), parts along dimension 0
- adapter_ids: int32 [128], P('data'), parts along dimension 0
- norm_gain: float32 [2560], replicated
- w_query: bfloat16 [2560, 32, 80], P(None, 'tensor')
- w_key: bfloat16 [2560, 32, 80], P(None, 'tensor')
- w_value: bfloat16 [2560, 32, 80], P(None, 'tensor')
- w_out: bfloat16 [32, 80, 2560], P('tensor')
- w_gate: bfloat16 [2560, 10240], P(None, 'tensor')
- w_up: bfloat16 [2560, 10240], P(None, 'tensor')
- w_down: bfloat16 [10240, 2560], P('tensor')
- lora_a_query: bfloat16 [4, 2560, 128], P(None, None, 'tensor')
- lora_b_query: bfloat16 [4, 128, 32, 80], P(None, None, 'tensor')
- lora_a_key: bfloat16 [4, 2560, 128], P(None, None, 'tensor')
- lora_b_key: bfloat16 [4, 128, 32, 80], P(None, None, 'tensor')
- lora_a_value: bfloat16 [4, 2560, 128], P(None, None, 'tensor')
- lora_b_value: bfloat16 [4, 128, 32, 80], P(None, None, 'tensor')
- lora_a_out: bfloat16 [4, 32, 80, 128], P(None, 'tensor')
- lora_b_out: bfloat16 [4, 128, 2560], P(None, None, 'tensor')
- lora_a_gate: bfloat16 [4, 2560, 128], P(None, None, 'tensor')
- lora_b_gate: bfloat16 [4, 128, 10240], P(None, None, 'tensor')
- lora_a_up: bfloat16 [4, 2560, 128], P(None, None, 'tensor')
- lora_b_up: bfloat16 [4, 128, 10240], P(None, None, 'tensor')
- lora_a_down: bfloat16 [4, 10240, 128], P(None, 'tensor')
- lora_b_down: bfloat16 [4, 128, 2560], P(None, None, 'tensor')
Outputs:
- output: bfloat16 [128, 32, 2560], P('data'), parts along dimension 0
There are 4 independent parts. A program takes and returns all parts, laid end to end along the dimension named above; an argument that names none is the same for every part.
All inputs are finite; a program needn't handle non-finite values.
Results may differ from a plain program's by a relative error of at most 0.014501.
Values are sent between devices in bfloat16 or wider.
A program may use at most 768 MiB of HBM per device.

v0:
```python
import jax
import jax.numpy as jnp
import math
from jax import lax
from jax.sharding import PartitionSpec as P

ALPHA = 16
EPS = 1e-5
ROPE_BASE = 10000.0


def rms_norm(x_blk, norm_gain):
    x_f32 = x_blk.astype(jnp.float32)
    return (x_f32 * lax.rsqrt(jnp.mean(x_f32 * x_f32, axis=-1, keepdims=True) + EPS) * norm_gain).astype(jnp.bfloat16)


def rope_tables(seq_len, head_dim):
    half_dim = head_dim // 2
    inv_freq = ROPE_BASE ** (-jnp.arange(half_dim, dtype=jnp.float32) / half_dim)
    angles = jnp.arange(seq_len, dtype=jnp.float32)[:, None] * inv_freq[None, :]
    return jnp.cos(angles)[:, None, :], jnp.sin(angles)[:, None, :]


def rope_rotate(vals, cos_t, sin_t):
    half_dim = vals.shape[-1] // 2
    first = vals[..., :half_dim]
    second = vals[..., half_dim:]
    return jnp.concatenate([first * cos_t - second * sin_t, second * cos_t + first * sin_t], axis=-1)


def causal_attention(query_rot, key_rot, value_heads):
    seq_len = query_rot.shape[1]
    head_dim = query_rot.shape[3]
    scores = jnp.einsum('bqhd,bkhd->bhqk', query_rot, key_rot, preferred_element_type=jnp.float32) / math.sqrt(head_dim)
    causal = jnp.arange(seq_len)[:, None] >= jnp.arange(seq_len)[None, :]
    probs_bf = jax.nn.softmax(jnp.where(causal, scores, -1e30), axis=-1).astype(jnp.bfloat16)
    return jnp.einsum('bhqk,bkhd->bqhd', probs_bf, value_heads, preferred_element_type=jnp.float32).astype(jnp.bfloat16)


def solution(mesh):
    batch_spec = P('data', None, None)
    head_cols = P(None, 'tensor', None)
    head_rows = P('tensor', None, None)
    ff_cols = P(None, 'tensor')
    ff_rows = P('tensor', None)
    last_split = P(None, None, 'tensor')
    b_heads = P(None, None, 'tensor', None)
    a_heads = P(None, 'tensor', None, None)
    in_specs = (batch_spec, P('data'), P(None), head_cols, head_cols, head_cols, head_rows, ff_cols, ff_cols, ff_rows, last_split, b_heads, last_split, b_heads, last_split, b_heads, a_heads, last_split, last_split, last_split, last_split, last_split, head_cols, last_split)

    def local_layer(x_blk, adapter_ids, norm_gain, w_query, w_key, w_value, w_out, w_gate, w_up, w_down, a_query, b_query, a_key, b_key, a_value, b_value, a_out, b_out, a_gate, b_gate, a_up, b_up, a_down, b_down):
        seq_len = x_blk.shape[1]
        rank = a_out.shape[-1]
        scale = ALPHA / rank
        normed = rms_norm(x_blk, norm_gain)
        cos_t, sin_t = rope_tables(seq_len, w_query.shape[-1])

        def gather_mid(a_stack):
            part_mid = jnp.einsum('bsd,bdr->bsr', normed, a_stack[adapter_ids], preferred_element_type=jnp.float32).astype(jnp.bfloat16)
            return lax.all_gather(part_mid, 'tensor', axis=2, tiled=True)

        def head_proj(weight, a_stack, b_stack):
            value_a8 = gather_mid(a_stack)
            base_out = jnp.einsum('bsd,dhe->bshe', normed, weight, preferred_element_type=jnp.float32)
            array_b8 = jnp.einsum('bsr,brhe->bshe', value_a8, b_stack[adapter_ids], preferred_element_type=jnp.float32)
            return base_out + scale * array_b8

        def ffn_proj(weight, a_stack, b_stack):
            value_a8 = gather_mid(a_stack)
            base_out = jnp.einsum('bsd,df->bsf', normed, weight, preferred_element_type=jnp.float32)
            array_b8 = jnp.einsum('bsr,brf->bsf', value_a8, b_stack[adapter_ids], preferred_element_type=jnp.float32)
            return base_out + scale * array_b8

        query_rot = rope_rotate(head_proj(w_query, a_query, b_query), cos_t, sin_t).astype(jnp.bfloat16)
        key_rot = rope_rotate(head_proj(w_key, a_key, b_key), cos_t, sin_t).astype(jnp.bfloat16)
        value_heads = head_proj(w_value, a_value, b_value).astype(jnp.bfloat16)
        attended = causal_attention(query_rot, key_rot, value_heads)
        mlp_mixed = (jax.nn.silu(ffn_proj(w_gate, a_gate, b_gate)) * ffn_proj(w_up, a_up, b_up)).astype(jnp.bfloat16)
        mid_out = lax.psum(jnp.einsum('bshe,bher->bsr', attended, a_out[adapter_ids], preferred_element_type=jnp.float32).astype(jnp.bfloat16), 'tensor')
        mid_down = lax.psum(jnp.einsum('bsf,bfr->bsr', mlp_mixed, a_down[adapter_ids], preferred_element_type=jnp.float32).astype(jnp.bfloat16), 'tensor')
        base_part = (jnp.einsum('bshe,hed->bsd', attended, w_out, preferred_element_type=jnp.float32) + jnp.einsum('bsf,fd->bsd', mlp_mixed, w_down, preferred_element_type=jnp.float32)).astype(jnp.bfloat16)
        base_sum = lax.psum_scatter(base_part, 'tensor', scatter_dimension=2, tiled=True)
        local_c8 = jnp.einsum('bsr,brd->bsd', mid_out, b_out[adapter_ids], preferred_element_type=jnp.float32) + jnp.einsum('bsr,brd->bsd', mid_down, b_down[adapter_ids], preferred_element_type=jnp.float32)
        share_width = base_sum.shape[2]
        x_share = lax.dynamic_slice_in_dim(x_blk, lax.axis_index('tensor') * share_width, share_width, axis=2)
        y_share = (x_share.astype(jnp.float32) + base_sum.astype(jnp.float32) + scale * local_c8).astype(jnp.bfloat16)
        return lax.all_gather(y_share, 'tensor', axis=2, tiled=True)

    return jax.shard_map(local_layer, mesh=mesh, in_specs=in_specs, out_specs=batch_spec, check_vma=False)
```

profile of v0, /device:TPU:21, one launch (start us, length us, event | category | flops | bytes accessed | tf_op | source)
XLA Modules:
  0.0 544.7 jit_solution(10729658650429720793)
XLA Ops:
  12.9 4.5 convolution_convert_fusion.4
  17.4 25.6 %all_gather.20 = bf16[32,32,128]{1,2,0:T(8,128)(2,1)} all-gather(bf16[32,32,8]{1,2,0:T(8,128)(2,1)S(1)} %convolution_convert_fusion.4), channel_id=1, replica_groups=mesh['data'=4,'tensor'=16] {'tensor'}, dimensions={2}, use_global_device_ids=true | all-gather | bytes 278528 | tf_op jit(solution)/shard_map/all_gather | solution.py:60
  44.8 5.4 fusion.5
  56.4 17.6 %all_gather.19 = bf16[32,32,128]{1,2,0:T(8,128)(2,1)} all-gather(bf16[32,32,8]{1,2,0:T(8,128)(2,1)S(1)} %convolution_convert_fusion.5), channel_id=1, replica_groups=mesh['data'=4,'tensor'=16] {'tensor'}, dimensions={2}, use_global_device_ids=true | all-gather | bytes 278528 | tf_op jit(solution)/shard_map/all_gather | solution.py:60
  75.8 5.3 fusion.7
  87.3 19.0 %all_gather.18 = bf16[32,32,128]{1,0,2:T(8,128)(2,1)} all-gather(bf16[32,32,8]{1,0,2:T(8,128)(2,1)S(1)} %copy.43), channel_id=1, replica_groups=mesh['data'=4,'tensor'=16] {'tensor'}, dimensions={2}, use_global_device_ids=true | all-gather | bytes 278528 | tf_op jit(solution)/shard_map/all_gather | solution.py:60
  108.1 5.3 fusion.9
  119.5 17.6 %all_gather.21 = bf16[32,32,128]{1,2,0:T(8,128)(2,1)} all-gather(bf16[32,32,8]{1,2,0:T(8,128)(2,1)S(1)} %convolution_convert_fusion.3), channel_id=1, replica_groups=mesh['data'=4,'tensor'=16] {'tensor'}, dimensions={2}, use_global_device_ids=true | all-gather | bytes 278528 | tf_op jit(solution)/shard_map/all_gather | solution.py:60
  137.1 4.7 gather_fusion.7
  147.9 19.1 %all_gather.22 = bf16[32,32,128]{1,2,0:T(8,128)(2,1)} all-gather(bf16[32,32,8]{1,2,0:T(8,128)(2,1)S(1)} %convolution_convert_fusion.2), channel_id=1, replica_groups=mesh['data'=4,'tensor'=16] {'tensor'}, dimensions={2}, use_global_device_ids=true | all-gather | bytes 278528 | tf_op jit(solution)/shard_map/all_gather | solution.py:60
  167.0 4.6 gather_fusion.9
  171.6 9.5 %fusion.13 = f32[32,32,640]{2,1,0:T(8,128)} fusion(bf16[2560,640]{1,0:T(8,128)(2,1)} %param.32, bf16[32,32,2560]{2,1,0:T(8,128)(2,1)} %param.24, f32[2560]{0:T(1024)S(1)} %copy-done.22, f32[32,32]{1,0:T(8,128)S(1)} %add_rsqrt_fusion), kind=kOutput, calls=%fused_computation.30 | convolution fusion | flops 3365928960 | bytes 11155456 | tf_op jit(solution)/shard_map/bsd,df->bsf/dot_general | solution.py:70
  181.1 8.3 %fusion.15 = f32[32,32,640]{2,1,0:T(8,128)} fusion(bf16[2560,640]{1,0:T(8,128)(2,1)S(1)} %copy-done.21, bf16[32,32,2560]{2,1,0:T(8,128)(2,1)} %param.24, f32[2560]{0:T(1024)S(1)} %copy-done.22, f32[32,32]{1,0:T(8,128)S(1)} %add_rsqrt_fusion), kind=kOutput, calls=%fused_computation.32 | convolution fusion | flops 3365928960 | bytes 11155456 | tf_op jit(solution)/shard_map/bsd,df->bsf/dot_general | solution.py:70
  191.2 4.7 gather_fusion.12
  195.9 5.5 %fusion.78 = f32[32,32,640]{2,1,0:T(8,128)} fusion(bf16[32,32,128]{1,2,0:T(8,128)(2,1)} %all_gather.21, bf16[32,128,640]{2,1,0:T(8,128)(2,1)} %gather_fusion.7), kind=kOutput, calls=%fused_computation.96 | convolution fusion | flops 167772160 | bytes 8126464 | tf_op jit(solution)/shard_map/bsr,brf->bsf/dot_general | solution.py:71
  209.3 4.5 fusion.27
  216.7 6.5 %multiply_convert_fusion = bf16[32,32,640]{2,1,0:T(8,128)(2,1)S(1)} fusion(f32[32,32,640]{2,1,0:T(8,128)} %fusion.13, f32[32,32,640]{2,1,0:T(8,128)} %fusion.15, f32[32,32,640]{2,1,0:T(8,128)} %fusion.78, bf16[32,32,128]{1,2,0:T(8,128)(2,1)} %all_gather.22, bf16[32,128,640]{2,1,0:T(8,128)(2,1)} %gather_fusion.9), kind=kOutput, calls=%fused_computation.34 | convolution fusion | flops 174325760 | bytes 14680064 | tf_op jit(solution)/shard_map/bsr,brf->bsf/dot_general | solution.py:71
  226.1 5.6 %fusion.11 = f32[32,32,2560]{2,1,0:T(8,128)S(1)} fusion(bf16[32,32,640]{2,1,0:T(8,128)(2,1)} %copy-done.16, bf16[640,2560]{1,0:T(8,128)(2,1)S(1)} %copy-done), kind=kOutput, calls=%fused_computation.28 | convolution fusion | flops 3355443200 | bytes 15073280 | tf_op jit(solution)/shard_map/bsf,fd->bsd/dot_general | solution.py:81
  235.7 28.3 %copy.37 = bf16[32,32,2560]{1,0,2:T(8,128)(2,1)} copy(bf16[32,32,2560]{2,1,0:T(8,128)(2,1)} %fusion.4) | data formatting | bytes 10485760
  264.0 28.7 %reshape.196 = bf16[2560,1024]{1,0:T(8,128)(2,1)} reshape(bf16[2560,32,32]{2,1,0:T(8,128)(2,1)} %bitcast.77) | data formatting | bytes 10485760
  298.1 30.3 %all-reduce.3.cloned.1.call-done = (bf16[32,32,128]{2,1,0:T(8,128)(2,1)}, bf16[32,32,128]{2,1,0:T(8,128)(2,1)}) async-done(((bf16[32,32,128]{2,1,0:T(8,128)(2,1)}, bf16[32,32,128]{2,1,0:T(8,128)(2,1)}), (bf16[32,32,128]{2,1,0:T(8,128)(2,1)}, bf16[32,32,128]{2,1,0:T(8,128)(2,1)})) %all-reduce.3.cloned.1.call-update) | async-done | bytes 524304 | tf_op jit(solution)/shard_map/psum | solution.py:79
  331.7 58.4 %reduce-scatter.4.cloned.1.call-done = bf16[160,1024]{1,0:T(8,128)(2,1)} async-done(((bf16[2560,1024]{1,0:T(8,128)(2,1)}), bf16[160,1024]{1,0:T(8,128)(2,1)}) %reduce-scatter.4.cloned.1.call-update) | async-done | bytes 327696
  402.3 114.1 %all-gather.2.cloned.1.call-done = bf16[32,32,2560]{1,0,2:T(8,128)(2,1)} async-done(((bf16[32,32,160]{1,0,2:T(8,128)(2,1)}), bf16[32,32,2560]{1,0,2:T(8,128)(2,1)}) %all-gather.2.cloned.1.call-update) | async-done | bytes 5242896 | tf_op jit(solution)/shard_map/all_gather | solution.py:87
  516.4 21.5 %copy.28 = bf16[32,32,2560]{2,1,0:T(8,128)(2,1)} copy(bf16[32,32,2560]{1,0,2:T(8,128)(2,1)} %all-gather.2.cloned.1.call-done) | data formatting | bytes 10485760 | tf_op jit(solution)/shard_map/all_gather | solution.py:87
  (92 shorter events, 76.6 us)
Async XLA Ops:
  6.5 219.5 %copy-start = (bf16[640,2560]{1,0:T(8,128)(2,1)S(1)}, bf16[640,2560]{1,0:T(8,128)(2,1)}, u32[]{:S(2)}) copy-start(bf16[640,2560]{1,0:T(8,128)(2,1)} %param.33) | copy-start | bytes 9830404
  6.6 321.9 %all-reduce.3.cloned.1.call-start = ((), (), s32[]{:S(2)}) async-start(), calls=%async_computation.3 | async-start | bytes 1048576 | tf_op jit(solution)/shard_map/psum | solution.py:79
  12.9 30.1 %copy-start.6 = (bf16[4,128,2,80]{1,3,2,0:T(8,128)(2,1)S(1)}, bf16[4,128,2,80]{1,3,2,0:T(8,128)(2,1)}, u32[]{:S(2)}) copy-start(bf16[4,128,2,80]{1,3,2,0:T(8,128)(2,1)} %param.37) | copy-start | bytes 491524
  44.8 5.4 copy-start.2
  51.9 22.0 %copy-start.7 = (bf16[4,128,2,80]{1,3,2,0:T(8,128)(2,1)S(1)}, bf16[4,128,2,80]{1,3,2,0:T(8,128)(2,1)}, u32[]{:S(2)}) copy-start(bf16[4,128,2,80]{1,3,2,0:T(8,128)(2,1)} %param.35) | copy-start | bytes 491524
  75.8 5.4 copy-start.3
  82.8 23.5 %copy-start.8 = (bf16[4,128,2,80]{1,3,2,0:T(8,128)(2,1)S(1)}, bf16[4,128,2,80]{1,3,2,0:T(8,128)(2,1)}, u32[]{:S(2)}) copy-start(bf16[4,128,2,80]{1,3,2,0:T(8,128)(2,1)} %param.39) | copy-start | bytes 491524
  108.1 5.3 copy-start.4
  137.1 4.7 copy-start.5
  171.6 9.5 %copy-start.21 = (bf16[2560,640]{1,0:T(8,128)(2,1)S(1)}, bf16[2560,640]{1,0:T(8,128)(2,1)}, u32[]{:S(2)}) copy-start(bf16[2560,640]{1,0:T(8,128)(2,1)} %param.31) | copy-start | bytes 9830404
  181.1 8.3 %copy-start.10 = (bf16[4,2,80,128]{3,2,1,0:T(8,128)(2,1)S(1)}, bf16[4,2,80,128]{3,2,1,0:T(8,128)(2,1)}, u32[]{:S(2)}) copy-start(bf16[4,2,80,128]{3,2,1,0:T(8,128)(2,1)} %param.40) | copy-start | bytes 491524
  195.9 5.5 %copy-start.11 = (bf16[32,128,2,80]{1,3,2,0:T(8,128)(2,1)S(1)}, bf16[32,128,2,80]{1,3,2,0:T(8,128)(2,1)}, u32[]{:S(2)}) copy-start(bf16[32,128,2,80]{1,3,2,0:T(8,128)(2,1)} %gather_fusion.5) | copy-start | bytes 3932164
  195.9 5.5 %copy-start.13 = (bf16[32,32,128]{1,2,0:T(8,128)(2,1)S(1)}, bf16[32,32,128]{1,2,0:T(8,128)(2,1)}, u32[]{:S(2)}) copy-start(bf16[32,32,128]{1,2,0:T(8,128)(2,1)} %all_gather.20) | copy-start | bytes 786436
  195.9 5.5 %copy-start.17 = (f32[32,32,2,80]{3,1,2,0:T(8,128)S(1)}, f32[32,32,2,80]{3,1,2,0:T(8,128)}, u32[]{:S(2)}) copy-start(f32[32,32,2,80]{3,1,2,0:T(8,128)} %fusion.5) | copy-start | bytes 1966084
  195.9 6.6 %copy-start.12 = (bf16[32,128,2,80]{1,3,2,0:T(8,128)(2,1)S(1)}, bf16[32,128,2,80]{1,3,2,0:T(8,128)(2,1)}, u32[]{:S(2)}) copy-start(bf16[32,128,2,80]{1,3,2,0:T(8,128)(2,1)} %gather_fusion.3) | copy-start | bytes 3932164
  195.9 6.7 %copy-start.14 = (bf16[32,32,128]{1,2,0:T(8,128)(2,1)S(1)}, bf16[32,32,128]{1,2,0:T(8,128)(2,1)}, u32[]{:S(2)}) copy-start(bf16[32,32,128]{1,2,0:T(8,128)(2,1)} %all_gather.19) | copy-start | bytes 786436
  195.9 6.7 %copy-start.18 = (f32[32,32,2,80]{3,1,2,0:T(8,128)S(1)}, f32[32,32,2,80]{3,1,2,0:T(8,128)}, u32[]{:S(2)}) copy-start(f32[32,32,2,80]{3,1,2,0:T(8,128)} %fusion.7) | copy-start | bytes 1966084
  213.8 10.4 %slice-start = ((s8[5242880]{0:T(1024)(128)(4,1)}), s8[4194304]{0:T(1024)(128)(4,1)S(1)}, s32[]{:S(2)}) async-start(s8[5242880]{0:T(1024)(128)(4,1)} %bitcast.78), calls=%async_computation.4 | async-start | bytes 8388608
  216.7 7.6 %slice-start.1 = ((s8[5242880]{0:T(1024)(128)(4,1)}), s8[1048576]{0:T(1024)(128)(4,1)S(1)}, s32[]{:S(2)}) async-start(s8[5242880]{0:T(1024)(128)(4,1)} %bitcast.78), calls=%async_computation.5 | async-start | bytes 2097152
  226.0 164.1 %reduce-scatter.4.cloned.1.call-start = ((), (), s32[]{:S(2)}) async-start(), calls=%async_computation.2 | async-start | bytes 5570560
  226.1 5.7 %copy-start.15 = (bf16[32,32,2,80]{3,1,2,0:T(8,128)(2,1)S(1)}, bf16[32,32,2,80]{3,1,2,0:T(8,128)(2,1)}, u32[]{:S(2)}) copy-start(bf16[32,32,2,80]{3,1,2,0:T(8,128)(2,1)} %fusion.27) | copy-start | bytes 983044
  226.1 5.7 %copy-start.19 = (bf16[2,80,2560]{2,1,0:T(8,128)(2,1)S(1)}, bf16[2,80,2560]{2,1,0:T(8,128)(2,1)}, u32[]{:S(2)}) copy-start(bf16[2,80,2560]{2,1,0:T(8,128)(2,1)} %param.30) | copy-start | bytes 2457604
  292.8 223.6 %all-gather.2.cloned.1.call-start = ((), (), s32[]{:S(2)}) async-start(), calls=%async_computation.1 | async-start | bytes 22282240 | tf_op jit(solution)/shard_map/all_gather | solution.py:87
  328.4 67.3 %copy-start.20 = (bf16[32,32,128]{2,1,0:T(8,128)(2,1)S(1)}, bf16[32,32,128]{2,1,0:T(8,128)(2,1)}, u32[]{:S(2)}) copy-start(bf16[32,32,128]{2,1,0:T(8,128)(2,1)} %get-tuple-element.6) | copy-start | bytes 786436
  (4 other events, 8.3 us)
Sparse Core Ops, SparseCore 0:
  226.1 102.2 all-reduce.2
  330.8 59.2 reduce-scatter.3
  402.4 113.9 all-gather.1
where the time goes:
time: 554 us; the launch traced here: 545 us
  waiting for transfers between devices  203 us (37%)
  local copies, waits for them, and re-layouts  123 us (22%)
  matrix products  99.4 us (18%)
  blocking collectives  98.8 us (18%)
  between operations  13.6 us (2%)
  other arithmetic  6.87 us (1%)
    all_gather x1, waiting for transfers between devices, local_layer(): return lax.all_gather(y_share, 'tensor', axis=2, tiled=True)  114 us
    all_gather x5, blocking collectives, gather_mid(): return lax.all_gather(part_mid, 'tensor', axis=2, tiled=True)  98.8 us
    unnamed x54, local copies, waits for them, and re-layouts  64.3 us
    unnamed x4, waiting for transfers between devices  58.5 us
    psum x1, waiting for transfers between devices, local_layer(): lax.psum(jnp.einsum('bshe,bher->bsr', attended, a_out[adapter_ids], prefe...  30.3 us
    dot_general x5, matrix products, gather_mid(): jnp.einsum('bsd,bdr->bsr', normed, a_stack[adapter_ids], preferred_elemen...  22.2 us
    all_gather x1, local copies, waits for them, and re-layouts, local_layer(): return lax.all_gather(y_share, 'tensor', axis=2, tiled=True)  21.5 us
    dot_general x2, matrix products, ffn_proj(): jnp.einsum('bsd,df->bsf', normed, weight, preferred_element_type=jnp.floa...  17.8 us
  transfers between devices with their start and end apart: 3, of which 3 were waited for; matrix products, arithmetic and copies ran while one was open for 14% of the time, Pallas kernels for 0%

commit v1 on v0

v1 whole, which is shorter than its diff:
```python
import functools
import math

import jax
import jax.numpy as jnp
import numpy as np
from jax import lax
from jax.experimental import pallas as pl
from jax.experimental.pallas import tpu as pltpu
from jax.sharding import PartitionSpec as P

ALPHA = 16
EPS = 1e-5
ROPE_BASE = 10000.0
MESH = pl.DeviceIdType.MESH
F32 = jnp.float32
BF16 = jnp.bfloat16
PASSES = 2


def mm(lhs, rhs, lc=1, rc=0):
    return lax.dot_general(lhs, rhs, (((lc,), (rc,)), ((), ())), preferred_element_type=F32)


def layer_kernel(cfg, x_hbm, ids_ref, gain_ref, cos_ref, sin_ref,
                 wq, wk, wv, wo, wg, wu, wd,
                 aq, ak, av, ag, au, bq, bk, bv, bg, bu,
                 ao, ad, bo, bd, y_hbm,
                 xv, hv, a_v, wqkv, wgu, bqkv, bgu, wo_v, wd_v, ao_v, ad_v, btg,
                 qkv_base, gu_base, gm, mmk, qk_v, ot_v, m_v, midp,
                 buf, drecv, ring, mg, basef, yv,
                 ld, mid_s, mid_r, md_s, md_r, bt_s, bt_r, dd_s, dd_r, rg_s, rg_r,
                 mg_s, mg_r, ag_s, ag_r, ad_s, ad_r, out_s):
    n, tokens, seq, n_adapt, rank, heads, head, ff = cfg
    chips = n // 2
    half = tokens // PASSES
    wide = heads * head
    share = rank // n
    scale = ALPHA / rank
    d_model = xv.shape[1]
    cols = d_model // (chips // 2)
    rows = half // 4
    mrows = 2 * rank // (chips // 2)
    me = lax.axis_index('tensor')
    chip = me // 2
    core = lax.rem(me, 2)
    sign = 1 - 2 * core
    partner = 2 * chip + 1 - core

    def wrap(c):
        return lax.rem(c + 2 * chips, chips)

    def dev(c):
        return 2 * wrap(c) + core

    def rcopy(src, dst, ssem, rsem, to):
        return pltpu.make_async_remote_copy(src_ref=src, dst_ref=dst, send_sem=ssem, recv_sem=rsem,
                                            device_id={'tensor': to}, device_id_type=MESH)

    loads = []

    def load(src, dst):
        cp = pltpu.make_async_copy(src, dst, ld.at[len(loads)])
        cp.start()
        loads.append(cp)
        return cp

    tile = tokens // 4
    x_ld = [load(x_hbm.at[pl.ds(i * tile, tile)], xv.at[pl.ds(i * tile, tile)]) for i in range(4)]
    a_ld = [load(src, a_v.at[pl.ds(i * n_adapt * share, n_adapt * share)]) for i, src in enumerate((aq, ak, av, ag, au))]

    barrier = pltpu.get_barrier_semaphore()
    for step in range(1, n):
        pl.semaphore_signal(barrier, inc=1, device_id={'tensor': lax.rem(me + step, n)}, device_id_type=MESH)

    w1_ld = [load(src, wqkv.at[pl.ds(i * wide, wide)]) for i, src in enumerate((wq, wk, wv))]
    w2_ld = [load(src, wgu.at[:, pl.ds(i * ff, ff)]) for i, src in enumerate((wg, wu))]

    nt = 128
    for i in range(4):
        x_ld[i].wait()

        def norm_tile(j, carry, i=i):
            r = pl.ds(pl.multiple_of(i * tile + j * nt, nt), nt)
            xf = xv[r, :].astype(F32)
            inv = lax.rsqrt(jnp.mean(xf * xf, axis=-1, keepdims=True) + EPS)
            hv[r, :] = (xf * inv * gain_ref[...]).astype(BF16)
            return carry
        lax.fori_loop(0, tile // nt, norm_tile, 0)

    for cp in a_ld:
        cp.wait()

    def mid_slot(hf, c, k):
        return gm.at[hf, 2 * wrap(c) + k]

    def mid_ring(hf, way, s):
        sg = sign if way == 0 else -sign
        slot = mid_slot(hf, chip - sg * s, core)
        return rcopy(slot, slot, mid_s.at[hf, way, s], mid_r.at[hf, way, s], dev(chip + sg))

    def mid_d2d(hf, i):
        if i == 0:
            c = chip
        elif i <= 4:
            c = chip - sign * i
        else:
            c = chip + sign * (i - 4)
        slot = mid_slot(hf, c, core)
        return rcopy(slot, slot, md_s.at[hf, i], md_r.at[hf, i], partner)

    hch = chips // 2

    def mid_service(hf, s):
        for way in range(2):
            last = hch - way
            if s < last:
                mid_ring(hf, way, s).wait_recv()
                if s + 1 < last:
                    mid_ring(hf, way, s + 1).start()
                mid_d2d(hf, (1 if way == 0 else 5) + s).start()

    def ids_of(start, size):
        return ids_ref[:, pl.ds(start, size)]

    for hf in range(PASSES):
        mids = mm(a_v[...], hv[pl.ds(hf * half, half), :], 1, 1)
        ids = ids_of(hf * half, half)
        out = []
        for st in range(5):
            acc = jnp.zeros((share, half), F32)
            for a in range(n_adapt):
                lo = (st * n_adapt + a) * share
                acc = jnp.where(ids == a, mids[lo:lo + share], acc)
            out.append(acc)
        out.append(jnp.zeros((share, half), F32))
        gm[hf, me] = jnp.concatenate(out, axis=0).astype(BF16)
        if hf == 0:
            pl.semaphore_wait(barrier, n - 1)
        mid_ring(hf, 0, 0).start()
        mid_ring(hf, 1, 0).start()
        mid_d2d(hf, 0).start()

    b_ld = []
    for i, src in enumerate((bq, bk, bv)):
        for a in range(n_adapt):
            b_ld.append(load(src.at[a], bqkv.at[pl.ds(i * wide, wide), pl.ds(a * rank, rank)]))
    b_ld += [load(src, bgu.at[:, pl.ds(i * ff, ff)]) for i, src in enumerate((bg, bu))]
    o_ld = [load(wo, wo_v), load(wd, wd_v)]
    for a in range(n_adapt):
        o_ld.append(load(ao.at[a], ao_v.at[:, pl.ds(a * rank, rank)]))
        o_ld.append(load(ad.at[a], ad_v.at[:, pl.ds(a * rank, rank)]))
    bt_rows = pl.ds(pl.multiple_of(lax.rem(me, 4) * wide, 16), wide)
    bt_ld = []
    for st, src in enumerate((bo, bd)):
        for a in range(n_adapt):
            bt_ld.append(load(src.at[a], btg.at[bt_rows, pl.ds((st * n_adapt + a) * rank, rank)]))

    def base_qkv(hf):
        r = pl.ds(hf * half, half)
        qkv_base[:, r] = mm(wqkv[...], hv[r, :], 1, 1)

    def base_gu(hf, part):
        r = pl.ds(hf * half, half)
        c = pl.ds(part * ff, ff)
        gu_base[r, c] = mm(hv[r, :], wgu[:, c])

    for cp in w1_ld:
        cp.wait()
    base_qkv(0)
    for cp in w2_ld:
        cp.wait()
    base_gu(0, 0)
    mid_service(0, 0)
    mid_service(1, 0)
    base_gu(0, 1)
    base_qkv(1)
    mid_service(0, 1)
    mid_service(1, 1)
    base_gu(1, 0)
    mid_service(0, 2)
    mid_service(1, 2)
    base_gu(1, 1)
    mid_service(0, 3)
    mid_service(1, 3)

    pair = chip + 1 - 2 * lax.rem(chip, 2)

    def bt_slot(dv):
        return btg.at[pl.ds(pl.multiple_of(lax.rem(dv, 4) * wide, 16), wide)]

    bt_out = rcopy(bt_slot(me), bt_slot(me), bt_s.at[0], bt_r.at[0], dev(pair))
    bt_d2d = rcopy(bt_slot(me), bt_slot(me), bt_s.at[1], bt_r.at[1], partner)
    bt_fwd = rcopy(bt_slot(dev(pair)), bt_slot(dev(pair)), bt_s.at[2], bt_r.at[2], partner)
    for cp in bt_ld:
        cp.wait()
    bt_out.start()
    bt_d2d.start()

    for cp in b_ld + o_ld:
        cp.wait()

    def build_mask(hf, st):
        ids = ids_of(hf * half, half)
        parts = [gm[hf, t].astype(F32)[st * share:(st + 1) * share] for t in range(n)]
        full = jnp.concatenate(parts, axis=0)
        for a in range(n_adapt):
            mmk[pl.ds(a * rank, rank), :] = jnp.where(ids == a, full, 0.0).astype(BF16)

    def attend(hf):
        for i in range(8):
            mid_d2d(hf, i).wait_recv()
        r = pl.ds(hf * half, half)
        hd = head // 2
        for st in range(3):
            build_mask(hf, st)
            w = pl.ds(st * wide, wide)
            z = qkv_base[w, r] + scale * mm(bqkv[w, :], mmk[...])
            if st < 2:
                out = []
                for h in range(heads):
                    first = z[h * head:h * head + hd]
                    second = z[h * head + hd:(h + 1) * head]
                    cs, sn = cos_ref[...], sin_ref[...]
                    out += [first * cs - second * sn, second * cs + first * sn]
                z = jnp.concatenate(out, axis=0)
            qk_v[w, :] = z.astype(BF16)
        blk = 256
        qi = lax.broadcasted_iota(jnp.int32, (blk, blk), 0)
        ki = lax.broadcasted_iota(jnp.int32, (blk, blk), 1)
        keep = (qi >= ki) & (qi // seq == ki // seq)
        for h in range(heads):
            for b in range(half // blk):
                c = pl.ds(b * blk, blk)
                qh = qk_v[pl.ds(h * head, head), c]
                kh = qk_v[pl.ds(wide + h * head, head), c]
                vh = qk_v[pl.ds(2 * wide + h * head, head), c]
                sc = mm(qh, kh, 0, 0) * (1.0 / math.sqrt(head))
                sc = jnp.where(keep, sc, -1e30)
                e = jnp.exp(sc - jnp.max(sc, axis=-1, keepdims=True))
                pr = (e * (1.0 / jnp.sum(e, axis=-1, keepdims=True))).astype(BF16)
                ot_v[pl.ds(h * head, head), pl.ds(hf * half + b * blk, blk)] = mm(vh, pr, 1, 1).astype(BF16)

    def pick(full, hf):
        ids = ids_of(hf * half, half)
        acc = jnp.zeros((rank, half), F32)
        for a in range(n_adapt):
            acc = jnp.where(ids == a, full[a * rank:(a + 1) * rank], acc)
        return acc.astype(BF16)

    def gated(hf):
        r = pl.ds(hf * half, half)
        for part in range(2):
            build_mask(hf, 3 + part)
            c = pl.ds(part * ff, ff)
            gu_base[r, c] = gu_base[r, c] + scale * mm(mmk[...], bgu[:, c], 0, 0)
        zg = gu_base[r, pl.ds(0, ff)]
        zu = gu_base[r, pl.ds(ff, ff)]
        m_v[r, :] = (zg / (1.0 + jnp.exp(-zg)) * zu).astype(BF16)
        midp[hf, pl.ds(0, rank), :] = pick(mm(ao_v[...], ot_v[:, r], 0, 0), hf)
        midp[hf, pl.ds(rank, rank), :] = pick(mm(ad_v[...], m_v[r, :], 0, 1), hf)

    def offset_of(i):
        mag = hch - (i + 1) // 2
        return mag * (2 * lax.rem(jnp.int32(i), 2) - 1)

    def d2d(p, i):
        return rcopy(buf.at[p, i, 1 - core], drecv.at[p, i], dd_s.at[p, i], dd_r.at[p, i], partner)

    def piece(p, i):
        e = wrap(chip + offset_of(i))
        odd = lax.rem(e, 2)
        grp = e // 2
        r0 = pl.multiple_of(p * half + odd * 2 * rows, 2 * rows)
        c = pl.ds(pl.multiple_of(grp * cols, 128), cols)
        val = mm(m_v[pl.ds(r0, 2 * rows), :], wd_v[:, c]) + mm(ot_v[:, pl.ds(r0, 2 * rows)], wo_v[:, c], 0, 0)
        for k in range(2):
            buf[p, i, k, pl.ds(0, rows), :] = val[k * rows:(k + 1) * rows].astype(BF16)
            mr = pl.ds(pl.multiple_of(grp * mrows, mrows), mrows)
            mc = pl.ds(pl.multiple_of((odd * 2 + k) * rows, rows), rows)
            blkm = midp[p, mr, mc]
            for b in range(mrows // 16):
                buf[p, i, k, pl.ds(rows, 16), pl.ds(b * rows, rows)] = blkm[b * 16:(b + 1) * 16]
            rest = cols - (mrows // 16) * rows
            buf[p, i, k, pl.ds(rows, 16), pl.ds(cols - rest, rest)] = jnp.zeros((16, rest), BF16)
        d2d(p, i).start()

    def pieces(p, lo, hi):
        def body(i, carry):
            piece(p, i)
            return carry
        lax.fori_loop(lo, hi, body, 0)

    def ring_copy(p, way, s, i):
        sg = sign if way == 0 else -sign
        return rcopy(buf.at[p, i, core], ring.at[p, way, s], rg_s.at[p, way, s], rg_r.at[p, way, s], dev(chip + sg))

    def ring_index(way, s):
        if way == 0:
            return 0 if s == 0 else 2 * s - 1 + core
        return 2 * s + 2 - core

    def ring_step(p, s):
        for way in range(2):
            last = hch - way
            if s >= last:
                continue
            i = ring_index(way, s)
            d2d(p, i).wait_recv()
            tot = buf[p, i, core].astype(F32) + drecv[p, i].astype(F32)
            if s > 0:
                ring_copy(p, way, s - 1, 0).wait_recv()
                tot = tot + ring[p, way, s - 1].astype(F32)
            buf[p, i, core] = tot.astype(BF16)
            ring_copy(p, way, s, i).start()

    def mg_copy(p, d):
        slot = mg.at[p, chip // 2]
        return rcopy(slot, slot, mg_s.at[p, d - 1], mg_r.at[p, d - 1], dev(chip + 2 * d))

    def finish_sum(p):
        i = 2 * hch - 1
        d2d(p, i).wait_recv()
        ring_copy(p, 0, hch - 1, 0).wait_recv()
        ring_copy(p, 1, hch - 2, 0).wait_recv()
        tot = (buf[p, i, core].astype(F32) + drecv[p, i].astype(F32)
               + ring[p, 0, hch - 1].astype(F32) + ring[p, 1, hch - 2].astype(F32))
        basef[p] = tot[:rows]
        tail = tot[rows:]
        for b in range(mrows // 16):
            mg[p, chip // 2, pl.ds(b * 16, 16), :] = tail[:, b * rows:(b + 1) * rows].astype(BF16)
        for d in range(1, hch):
            mg_copy(p, d).start()

    def y_slot(p, c, k):
        c = wrap(c)
        r0 = pl.multiple_of(p * half + (2 * lax.rem(c, 2) + k) * rows, rows)
        return yv.at[pl.ds(r0, rows), pl.ds(pl.multiple_of((c // 2) * cols, 128), cols)]

    def ag_ring(p, way, s):
        sg = sign if way == 0 else -sign
        slot = y_slot(p, chip - sg * s, core)
        return rcopy(slot, slot, ag_s.at[p, way, s], ag_r.at[p, way, s], dev(chip + sg))

    def ag_d2d(p, i):
        if i == 0:
            c = chip
        elif i <= 4:
            c = chip - sign * i
        else:
            c = chip + sign * (i - 4)
        slot = y_slot(p, c, core)
        return rcopy(slot, slot, ad_s.at[p, i], ad_r.at[p, i], partner)

    def ag_service(p, s):
        for way in range(2):
            last = hch - way
            if s < last:
                ag_ring(p, way, s).wait_recv()
                if s + 1 < last:
                    ag_ring(p, way, s + 1).start()
                ag_d2d(p, (1 if way == 0 else 5) + s).start()

    def finish_y(p):
        for d in range(1, hch):
            mg_copy(p, d).wait_recv()
        q = 2 * lax.rem(chip, 2) + core
        t0 = pl.multiple_of(p * half + q * rows, rows)
        c0 = pl.ds(pl.multiple_of((chip // 2) * cols, 128), cols)
        ids = ids_of(t0, rows)
        mids = jnp.concatenate([mg[p, g].astype(F32) for g in range(hch)], axis=0)
        parts = []
        for st in range(2):
            for a in range(n_adapt):
                parts.append(jnp.where(ids == a, mids[st * rank:(st + 1) * rank], 0.0).astype(BF16))
        lora = mm(jnp.concatenate(parts, axis=0), btg[...], 0, 1)
        xs = xv[pl.ds(t0, rows), c0].astype(F32)
        yv[pl.ds(t0, rows), c0] = (xs + basef[p] + scale * lora).astype(BF16)
        ag_ring(p, 0, 0).start()
        ag_ring(p, 1, 0).start()
        ag_d2d(p, 0).start()

    def out_copy(p):
        r = pl.ds(p * half, half)
        return pltpu.make_async_copy(yv.at[r], y_hbm.at[r], out_s.at[p])

    def finish_out(p):
        for i in range(8):
            ag_d2d(p, i).wait_recv()
        out_copy(p).start()

    attend(0)
    gated(0)
    bt_out.wait_recv()
    bt_fwd.start()
    pieces(0, 0, 3)
    ring_step(0, 0)
    pieces(0, 3, 8)
    attend(1)
    ring_step(0, 1)
    gated(1)
    pieces(1, 0, 3)
    ring_step(1, 0)
    ring_step(0, 2)
    pieces(1, 3, 8)
    ring_step(1, 1)
    ring_step(0, 3)
    ring_step(1, 2)
    bt_d2d.wait_recv()
    bt_fwd.wait_recv()
    finish_sum(0)
    ring_step(1, 3)
    finish_y(0)
    finish_sum(1)
    ag_service(0, 0)
    finish_y(1)
    ag_service(0, 1)
    ag_service(1, 0)
    ag_service(0, 2)
    ag_service(1, 1)
    ag_service(0, 3)
    ag_service(1, 2)
    finish_out(0)
    ag_service(1, 3)
    finish_out(1)

    for p in range(PASSES):
        for i in range(8):
            mid_d2d(p, i).wait_send()
            d2d(p, i).wait_send()
            ag_d2d(p, i).wait_send()
        for way in range(2):
            for s in range(hch - way):
                mid_ring(p, way, s).wait_send()
                ring_copy(p, way, s, 0).wait_send()
                ag_ring(p, way, s).wait_send()
        for d in range(1, hch):
            mg_copy(p, d).wait_send()
        out_copy(p).wait()
    bt_out.wait_send()
    bt_d2d.wait_send()
    bt_fwd.wait_send()


def solution(mesh):
    n = mesh.shape['tensor']
    batch_spec = P('data', None, None)
    head_cols = P(None, 'tensor', None)
    head_rows = P('tensor', None, None)
    ff_cols = P(None, 'tensor')
    ff_rows = P('tensor', None)
    last_split = P(None, None, 'tensor')
    b_heads = P(None, None, 'tensor', None)
    a_heads = P(None, 'tensor', None, None)
    in_specs = (batch_spec, P('data'), P(None), head_cols, head_cols, head_cols, head_rows, ff_cols, ff_cols, ff_rows, last_split, b_heads, last_split, b_heads, last_split, b_heads, a_heads, last_split, last_split, last_split, last_split, last_split, head_cols, last_split)

    def local_layer(x_blk, adapter_ids, norm_gain, w_query, w_key, w_value, w_out, w_gate, w_up, w_down, a_query, b_query, a_key, b_key, a_value, b_value, a_out, b_out, a_gate, b_gate, a_up, b_up, a_down, b_down):
        seqs, seq, d_model = x_blk.shape
        tokens = seqs * seq
        n_adapt, _, rank = a_down.shape
        heads, head = w_query.shape[1:]
        wide = heads * head
        ff = w_gate.shape[1]
        chips = n // 2
        half = tokens // PASSES
        rows = half // 4
        cols = d_model // (chips // 2)
        mrows = 2 * rank // (chips // 2)
        share = rank // n

        ids = jnp.repeat(adapter_ids, seq).reshape(1, tokens)
        hd = head // 2
        inv_freq = ROPE_BASE ** (-np.arange(hd, dtype=np.float32) / np.float32(hd))
        ang = inv_freq[:, None] * np.arange(seq, dtype=np.float32)[None, :]
        ang = np.tile(ang.astype(np.float32), (1, half // seq))
        cos_t, sin_t = jnp.asarray(np.cos(ang), F32), jnp.asarray(np.sin(ang), F32)

        def wt(w):
            return w.transpose(1, 2, 0).reshape(wide, d_model)

        def at(a):
            return a.transpose(0, 2, 1).reshape(n_adapt * share, d_model)

        def bt(b):
            return b.transpose(0, 2, 3, 1).reshape(n_adapt, wide, rank)

        args = (x_blk.reshape(tokens, d_model), ids, norm_gain.reshape(1, d_model), cos_t, sin_t,
                wt(w_query), wt(w_key), wt(w_value), w_out.reshape(wide, d_model), w_gate, w_up, w_down,
                at(a_query), at(a_key), at(a_value), at(a_gate), at(a_up),
                bt(b_query), bt(b_key), bt(b_value), b_gate.reshape(n_adapt * rank, ff), b_up.reshape(n_adapt * rank, ff),
                a_out.reshape(n_adapt, wide, rank), a_down, b_out.transpose(0, 2, 1), b_down.transpose(0, 2, 1))
        hbm = pl.BlockSpec(memory_space=pl.ANY)
        vmem = pl.BlockSpec(memory_space=pltpu.VMEM)
        dma = pltpu.SemaphoreType.DMA
        cfg = (n, tokens, seq, n_adapt, rank, heads, head, ff)
        scratch = [
            pltpu.VMEM((tokens, d_model), BF16),
            pltpu.VMEM((tokens, d_model), BF16),
            pltpu.VMEM((5 * n_adapt * share, d_model), BF16),
            pltpu.VMEM((3 * wide, d_model), BF16),
            pltpu.VMEM((d_model, 2 * ff), BF16),
            pltpu.VMEM((3 * wide, n_adapt * rank), BF16),
            pltpu.VMEM((n_adapt * rank, 2 * ff), BF16),
            pltpu.VMEM((wide, d_model), BF16),
            pltpu.VMEM((ff, d_model), BF16),
            pltpu.VMEM((wide, n_adapt * rank), BF16),
            pltpu.VMEM((ff, n_adapt * rank), BF16),
            pltpu.VMEM((4 * wide, 2 * n_adapt * rank), BF16),
            pltpu.VMEM((3 * wide, tokens), F32),
            pltpu.VMEM((tokens, 2 * ff), F32),
            pltpu.VMEM((PASSES, n, 6 * share, half), BF16),
            pltpu.VMEM((n_adapt * rank, half), BF16),
            pltpu.VMEM((3 * wide, half), BF16),
            pltpu.VMEM((wide, tokens), BF16),
            pltpu.VMEM((tokens, ff), BF16),
            pltpu.VMEM((PASSES, 2 * rank, half), BF16),
            pltpu.VMEM((PASSES, chips, 2, rows + 16, cols), BF16),
            pltpu.VMEM((PASSES, chips, rows + 16, cols), BF16),
            pltpu.VMEM((PASSES, 2, chips // 2, rows + 16, cols), BF16),
            pltpu.VMEM((PASSES, chips // 2, mrows, rows), BF16),
            pltpu.VMEM((PASSES, rows, cols), F32),
            pltpu.VMEM((tokens, d_model), BF16),
            dma((48,)),
            dma((PASSES, 2, 4)), dma((PASSES, 2, 4)), dma((PASSES, 8)), dma((PASSES, 8)),
            dma((3,)), dma((3,)), dma((PASSES, 8)), dma((PASSES, 8)),
            dma((PASSES, 2, 4)), dma((PASSES, 2, 4)), dma((PASSES, 3)), dma((PASSES, 3)),
            dma((PASSES, 2, 4)), dma((PASSES, 2, 4)), dma((PASSES, 8)), dma((PASSES, 8)),
            dma((PASSES,)),
        ]
        y = pl.pallas_call(
            functools.partial(layer_kernel, cfg),
            out_shape=jax.ShapeDtypeStruct((tokens, d_model), BF16),
            in_specs=[hbm] + [vmem] * 4 + [hbm] * 21,
            out_specs=hbm,
            scratch_shapes=scratch,
            compiler_params=pltpu.CompilerParams(collective_id=0, has_side_effects=True,
                                                 vmem_limit_bytes=67_000_000),
        )(*args)
        return y.reshape(x_blk.shape)

    return jax.shard_map(local_layer, mesh=mesh, in_specs=in_specs, out_specs=batch_spec, check_vma=False)
```

time: 554 us -> 118 us (0.21); the launches traced: 545 us -> 118 us
  waiting for transfers between devices: 203 us -> 0 us
  local copies, waits for them, and re-layouts: 123 us -> 8.09 us
  Pallas kernels: 0 us -> 110 us
  matrix products: 99.4 us -> 0 us
  blocking collectives: 98.8 us -> 0 us
  between operations: 13.6 us -> 0.01 us
  other arithmetic: 6.87 us -> 0 us
    all_gather x1 -> x0, waiting for transfers between devices: 114 us -> none  [local_layer(): return lax.all_gather(y_share, 'tensor', axis=2, tiled=True)]
    pallas_call x0 -> x1, Pallas kernels: none -> 110 us  [local_layer(): pl.pallas_call(functools.partial(layer_kernel, cfg), out_shape=jax.ShapeD...]
    all_gather x5 -> x0, blocking collectives: 98.8 us -> none  [gather_mid(): return lax.all_gather(part_mid, 'tensor', axis=2, tiled=True)]
    dot_general x21 -> x0, matrix products: 96 us -> none  [the longest x5 22.2 us: gather_mid(): jnp.einsum('bsd,bdr->bsr', normed, a_stack[adapter_ids], preferred_elemen...]
    unnamed x54 -> x1, local copies, waits for them, and re-layouts: 64.3 us -> 5.39 us
    unnamed x4 -> x0, waiting for transfers between devices: 58.5 us -> none
    gather x14 -> x0, local copies, waits for them, and re-layouts: 34.1 us -> none  [the longest x2 9.29 us: ffn_proj(): b_stack[adapter_ids]]
    psum x1 -> x0, waiting for transfers between devices: 30.3 us -> none  [local_layer(): lax.psum(jnp.einsum('bshe,bher->bsr', attended, a_out[adapter_ids], prefe...]
  transfers between devices with their start and end apart: 3 -> 0, of which waited for: 3 -> 0; matrix products, arithmetic and copies ran while one was open for 14% -> 0% of each run, Pallas kernels for 0% -> 0%
where the time goes in v1:
time: 118 us
  Pallas kernels  110 us (93%)
  local copies, waits for them, and re-layouts  8.09 us (7%)
    pallas_call x1, Pallas kernels, local_layer(): pl.pallas_call(functools.partial(layer_kernel, cfg), out_shape=jax.ShapeD...  110 us
    unnamed x1, local copies, waits for them, and re-layouts  5.39 us

profile of v1, /device:TPU:21, one launch (start us, length us, event | category | flops | bytes accessed | tf_op | source)
XLA Modules:
  0.0 117.6 jit_solution(16140232694602161027)
XLA Ops:
  0.0 1.3 %reshape.55.gain_ref = f32[1,2560]{1,0:T(1,128)} reshape(f32[2560]{0:T(1024)} %param.28) | data formatting | bytes 20480 | tf_op jit(solution)/shard_map/reshape | solution.py:487
  1.3 0.7 broadcast_in_dim.3
  2.0 0.7 reshape_reshape.3.ids_ref
  2.7 109.5 %shard_map.244 = bf16[1024,2560]{1,0:T(8,128)(2,1)} custom-call(bf16[1024,2560]{1,0:T(8,128)(2,1)} %bitcast.42, s32[1,1024]{1,0:T(1,128)} %reshape_reshape.3.ids_ref, f32[1,2560]{1,0:T(1,128)} %reshape.55.gain_ref, f32[40,512]{1,0:T(8,128)} %constant.4.clone.cos_ref, f32[40,512]{1,0:T(8,128)} %constant.5.clone.sin_ref, bf16[160,2560]{1,0:T(8,128)(2,1)} %bitcast.43, ...), custom_call_target="tpu_custom_call" | custom-call | tf_op jit(solution)/shard_map/pallas_call | solution.py:530
  112.3 5.4 %copy.28 = bf16[32,32,2560]{2,1,0:T(8,128)(2,1)} copy(bf16[32,32,2560]{2,1,0:T(8,128)(2,1)} %bitcast.41) | data formatting | bytes 10485760

commit v2 on v1

--- a/solution.py
+++ b/solution.py
@@ -16,21 +16,22 @@
 F32 = jnp.float32
 BF16 = jnp.bfloat16
 PASSES = 2
+SUBS = 2
 
 
 def mm(lhs, rhs, lc=1, rc=0):
     return lax.dot_general(lhs, rhs, (((lc,), (rc,)), ((), ())), preferred_element_type=F32)
 
 
-def layer_kernel(cfg, x_hbm, ids_ref, gain_ref, cos_ref, sin_ref,
+def layer_kernel(cfg, x_hbm, ids_hbm, gain_hbm, cos_hbm, sin_hbm,
                  wq, wk, wv, wo, wg, wu, wd,
                  aq, ak, av, ag, au, bq, bk, bv, bg, bu,
-                 ao, ad, bo, bd, y_hbm,
-                 xv, hv, a_v, wqkv, wgu, bqkv, bgu, wo_v, wd_v, ao_v, ad_v, btg,
-                 qkv_base, gu_base, gm, mmk, qk_v, ot_v, m_v, midp,
-                 buf, drecv, ring, mg, basef, yv,
+                 ao, ad, bo, bd, yv,
+                 ids_s, ids_ref, gain_v, gain_ref, cos_ref, sin_ref, xv, hv, a_v, wqkv, wgu, bqkv, bgu, wo_v, wd_v, ao_v, ad_v, btg,
+                 qkv_base, gu_base, gm, mmk, qk_v, ot_v, m_v, midp, midr, midx,
+                 buf, drecv, ring, mg, xo,
                  ld, mid_s, mid_r, md_s, md_r, bt_s, bt_r, dd_s, dd_r, rg_s, rg_r,
-                 mg_s, mg_r, ag_s, ag_r, ad_s, ad_r, out_s):
+                 mp_s, mp_r, mx_s, mx_r, mg_s, mg_r, ag_s, ag_r, ad_s, ad_r):
     n, tokens, seq, n_adapt, rank, heads, head, ff = cfg
     chips = n // 2
     half = tokens // PASSES
@@ -66,6 +67,7 @@
         return cp
 
     tile = tokens // 4
+    g_ld = [load(ids_hbm, ids_s), load(gain_hbm, gain_v)]
     x_ld = [load(x_hbm.at[pl.ds(i * tile, tile)], xv.at[pl.ds(i * tile, tile)]) for i in range(4)]
     a_ld = [load(src, a_v.at[pl.ds(i * n_adapt * share, n_adapt * share)]) for i, src in enumerate((aq, ak, av, ag, au))]
 
@@ -75,6 +77,16 @@
 
     w1_ld = [load(src, wqkv.at[pl.ds(i * wide, wide)]) for i, src in enumerate((wq, wk, wv))]
     w2_ld = [load(src, wgu.at[:, pl.ds(i * ff, ff)]) for i, src in enumerate((wg, wu))]
+
+    c_ld = [load(cos_hbm, cos_ref), load(sin_hbm, sin_ref)]
+    for cp in g_ld:
+        cp.wait()
+    where_seq = lax.broadcasted_iota(jnp.int32, (1, tokens), 1) // seq
+    ids_all = jnp.zeros((1, tokens), jnp.int32)
+    for b in range(tokens // seq):
+        ids_all = jnp.where(where_seq == b, ids_s[b], ids_all)
+    ids_ref[...] = ids_all
+    gain_ref[...] = jnp.concatenate([gain_v[b:b + 1, :] for b in range(gain_v.shape[0])], axis=1)
 
     nt = 128
     for i in range(4):
@@ -165,25 +177,6 @@
         c = pl.ds(part * ff, ff)
         gu_base[r, c] = mm(hv[r, :], wgu[:, c])
 
-    for cp in w1_ld:
-        cp.wait()
-    base_qkv(0)
-    for cp in w2_ld:
-        cp.wait()
-    base_gu(0, 0)
-    mid_service(0, 0)
-    mid_service(1, 0)
-    base_gu(0, 1)
-    base_qkv(1)
-    mid_service(0, 1)
-    mid_service(1, 1)
-    base_gu(1, 0)
-    mid_service(0, 2)
-    mid_service(1, 2)
-    base_gu(1, 1)
-    mid_service(0, 3)
-    mid_service(1, 3)
-
     pair = chip + 1 - 2 * lax.rem(chip, 2)
 
     def bt_slot(dv):
@@ -192,14 +185,6 @@
     bt_out = rcopy(bt_slot(me), bt_slot(me), bt_s.at[0], bt_r.at[0], dev(pair))
     bt_d2d = rcopy(bt_slot(me), bt_slot(me), bt_s.at[1], bt_r.at[1], partner)
     bt_fwd = rcopy(bt_slot(dev(pair)), bt_slot(dev(pair)), bt_s.at[2], bt_r.at[2], partner)
-    for cp in bt_ld:
-        cp.wait()
-    bt_out.start()
-    bt_d2d.start()
-
-    for cp in b_ld + o_ld:
-        cp.wait()
-
     def build_mask(hf, st):
         ids = ids_of(hf * half, half)
         parts = [gm[hf, t].astype(F32)[st * share:(st + 1) * share] for t in range(n)]
@@ -257,8 +242,35 @@
         zg = gu_base[r, pl.ds(0, ff)]
         zu = gu_base[r, pl.ds(ff, ff)]
         m_v[r, :] = (zg / (1.0 + jnp.exp(-zg)) * zu).astype(BF16)
-        midp[hf, pl.ds(0, rank), :] = pick(mm(ao_v[...], ot_v[:, r], 0, 0), hf)
-        midp[hf, pl.ds(rank, rank), :] = pick(mm(ad_v[...], m_v[r, :], 0, 1), hf)
+        for st, acc in enumerate((pick(mm(ao_v[...], ot_v[:, r], 0, 0), hf), pick(mm(ad_v[...], m_v[r, :], 0, 1), hf))):
+            for q in range(4):
+                midp[hf, q % 2, q // 2, pl.ds(st * rank, rank), :] = acc[:, q * rows:(q + 1) * rows]
+        mid_part(hf).start()
+
+    def mid_part(p):
+        return rcopy(midp.at[p, 1 - core], midr.at[p], mp_s.at[p], mp_r.at[p], partner)
+
+    def mid_block(p, c):
+        c = wrap(c)
+        return midp.at[p, core, lax.rem(c, 2), pl.ds(pl.multiple_of((c // 2) * mrows, mrows), mrows)]
+
+    def mid_send(p, d):
+        return rcopy(mid_block(p, chip + d), midx.at[p, d - 1], mx_s.at[p, d - 1], mx_r.at[p, d - 1], dev(chip + d))
+
+    def mid_scatter(p):
+        mid_part(p).wait_recv()
+        midp[p, core] = (midp[p, core].astype(F32) + midr[p].astype(F32)).astype(BF16)
+        for d in (4, 3, 5, 2, 6, 1, 7):
+            mid_send(p, d).start()
+
+    def mid_gather(p):
+        tot = mid_block(p, chip)[...].astype(F32)
+        for d in range(1, chips):
+            mid_send(p, d).wait_recv()
+            tot = tot + midx[p, d - 1].astype(F32)
+        mg[p, chip // 2] = tot.astype(BF16)
+        for d in range(1, hch):
+            mg_copy(p, d).start()
 
     def offset_of(i):
         mag = hch - (i + 1) // 2
@@ -275,14 +287,7 @@
         c = pl.ds(pl.multiple_of(grp * cols, 128), cols)
         val = mm(m_v[pl.ds(r0, 2 * rows), :], wd_v[:, c]) + mm(ot_v[:, pl.ds(r0, 2 * rows)], wo_v[:, c], 0, 0)
         for k in range(2):
-            buf[p, i, k, pl.ds(0, rows), :] = val[k * rows:(k + 1) * rows].astype(BF16)
-            mr = pl.ds(pl.multiple_of(grp * mrows, mrows), mrows)
-            mc = pl.ds(pl.multiple_of((odd * 2 + k) * rows, rows), rows)
-            blkm = midp[p, mr, mc]
-            for b in range(mrows // 16):
-                buf[p, i, k, pl.ds(rows, 16), pl.ds(b * rows, rows)] = blkm[b * 16:(b + 1) * 16]
-            rest = cols - (mrows // 16) * rows
-            buf[p, i, k, pl.ds(rows, 16), pl.ds(cols - rest, rest)] = jnp.zeros((16, rest), BF16)
+            buf[p, i, k] = val[k * rows:(k + 1) * rows].astype(BF16)
         d2d(p, i).start()
 
     def pieces(p, lo, hi):
@@ -291,9 +296,13 @@
             return carry
         lax.fori_loop(lo, hi, body, 0)
 
-    def ring_copy(p, way, s, i):
+    def sub(u):
+        return pl.ds(u * (rows // SUBS), rows // SUBS)
+
+    def ring_copy(p, way, s, u, i):
         sg = sign if way == 0 else -sign
-        return rcopy(buf.at[p, i, core], ring.at[p, way, s], rg_s.at[p, way, s], rg_r.at[p, way, s], dev(chip + sg))
+        return rcopy(buf.at[p, i, core, sub(u)], ring.at[p, way, s, sub(u)],
+                     rg_s.at[p, way, s, u], rg_r.at[p, way, s, u], dev(chip + sg))
 
     def ring_index(way, s):
         if way == 0:
@@ -301,142 +310,167 @@
         return 2 * s + 2 - core
 
     def ring_step(p, s):
-        for way in range(2):
-            last = hch - way
-            if s >= last:
-                continue
-            i = ring_index(way, s)
-            d2d(p, i).wait_recv()
-            tot = buf[p, i, core].astype(F32) + drecv[p, i].astype(F32)
-            if s > 0:
-                ring_copy(p, way, s - 1, 0).wait_recv()
-                tot = tot + ring[p, way, s - 1].astype(F32)
-            buf[p, i, core] = tot.astype(BF16)
-            ring_copy(p, way, s, i).start()
+        for u in range(SUBS):
+            for way in range(2):
+                last = hch - way
+                if s >= last:
+                    continue
+                i = ring_index(way, s)
+                if u == 0:
+                    d2d(p, i).wait_recv()
+                tot = buf[p, i, core, sub(u)].astype(F32) + drecv[p, i, sub(u)].astype(F32)
+                if s > 0:
+                    ring_copy(p, way, s - 1, u, 0).wait_recv()
+                    tot = tot + ring[p, way, s - 1, sub(u)].astype(F32)
+                buf[p, i, core, sub(u)] = tot.astype(BF16)
+                ring_copy(p, way, s, u, i).start()
 
     def mg_copy(p, d):
         slot = mg.at[p, chip // 2]
         return rcopy(slot, slot, mg_s.at[p, d - 1], mg_r.at[p, d - 1], dev(chip + 2 * d))
 
-    def finish_sum(p):
-        i = 2 * hch - 1
-        d2d(p, i).wait_recv()
-        ring_copy(p, 0, hch - 1, 0).wait_recv()
-        ring_copy(p, 1, hch - 2, 0).wait_recv()
-        tot = (buf[p, i, core].astype(F32) + drecv[p, i].astype(F32)
-               + ring[p, 0, hch - 1].astype(F32) + ring[p, 1, hch - 2].astype(F32))
-        basef[p] = tot[:rows]
-        tail = tot[rows:]
-        for b in range(mrows // 16):
-            mg[p, chip // 2, pl.ds(b * 16, 16), :] = tail[:, b * rows:(b + 1) * rows].astype(BF16)
-        for d in range(1, hch):
-            mg_copy(p, d).start()
-
-    def y_slot(p, c, k):
+    def y_rows(p, c, k, u):
         c = wrap(c)
-        r0 = pl.multiple_of(p * half + (2 * lax.rem(c, 2) + k) * rows, rows)
-        return yv.at[pl.ds(r0, rows), pl.ds(pl.multiple_of((c // 2) * cols, 128), cols)]
-
-    def ag_ring(p, way, s):
+        return pl.multiple_of(p * half + (2 * lax.rem(c, 2) + k) * rows + u * (rows // SUBS), rows // SUBS)
+
+    def y_cols(c):
+        return pl.ds(pl.multiple_of((wrap(c) // 2) * cols, 128), cols)
+
+    def y_slot(p, c, k, u):
+        return yv.at[pl.ds(y_rows(p, c, k, u), rows // SUBS), y_cols(c)]
+
+    def ag_ring(p, way, s, u):
         sg = sign if way == 0 else -sign
-        slot = y_slot(p, chip - sg * s, core)
-        return rcopy(slot, slot, ag_s.at[p, way, s], ag_r.at[p, way, s], dev(chip + sg))
-
-    def ag_d2d(p, i):
+        slot = y_slot(p, chip - sg * s, core, u)
+        return rcopy(slot, slot, ag_s.at[p, way, s, u], ag_r.at[p, way, s, u], dev(chip + sg))
+
+    def ag_d2d(p, i, u):
         if i == 0:
             c = chip
         elif i <= 4:
             c = chip - sign * i
         else:
             c = chip + sign * (i - 4)
-        slot = y_slot(p, c, core)
-        return rcopy(slot, slot, ad_s.at[p, i], ad_r.at[p, i], partner)
+        slot = y_slot(p, c, core, u)
+        return rcopy(slot, slot, ad_s.at[p, i, u], ad_r.at[p, i, u], partner)
 
     def ag_service(p, s):
-        for way in range(2):
-            last = hch - way
-            if s < last:
-                ag_ring(p, way, s).wait_recv()
-                if s + 1 < last:
-                    ag_ring(p, way, s + 1).start()
-                ag_d2d(p, (1 if way == 0 else 5) + s).start()
-
-    def finish_y(p):
+        for u in range(SUBS):
+            for way in range(2):
+                last = hch - way
+                if s < last:
+                    ag_ring(p, way, s, u).wait_recv()
+                    if s + 1 < last:
+                        ag_ring(p, way, s + 1, u).start()
+                    ag_d2d(p, (1 if way == 0 else 5) + s, u).start()
+
+    def lora_out(p):
         for d in range(1, hch):
             mg_copy(p, d).wait_recv()
-        q = 2 * lax.rem(chip, 2) + core
-        t0 = pl.multiple_of(p * half + q * rows, rows)
-        c0 = pl.ds(pl.multiple_of((chip // 2) * cols, 128), cols)
-        ids = ids_of(t0, rows)
+        ids = ids_of(y_rows(p, chip, core, 0), rows)
         mids = jnp.concatenate([mg[p, g].astype(F32) for g in range(hch)], axis=0)
         parts = []
         for st in range(2):
             for a in range(n_adapt):
                 parts.append(jnp.where(ids == a, mids[st * rank:(st + 1) * rank], 0.0).astype(BF16))
         lora = mm(jnp.concatenate(parts, axis=0), btg[...], 0, 1)
-        xs = xv[pl.ds(t0, rows), c0].astype(F32)
-        yv[pl.ds(t0, rows), c0] = (xs + basef[p] + scale * lora).astype(BF16)
-        ag_ring(p, 0, 0).start()
-        ag_ring(p, 1, 0).start()
-        ag_d2d(p, 0).start()
-
-    def out_copy(p):
-        r = pl.ds(p * half, half)
-        return pltpu.make_async_copy(yv.at[r], y_hbm.at[r], out_s.at[p])
-
-    def finish_out(p):
-        for i in range(8):
-            ag_d2d(p, i).wait_recv()
-        out_copy(p).start()
-
+        r = pl.ds(y_rows(p, chip, core, 0), rows)
+        xo[p] = xv[r, y_cols(chip)].astype(F32) + scale * lora
+
+    def finish_y(p):
+        i = 2 * hch - 1
+        d2d(p, i).wait_recv()
+        for u in range(SUBS):
+            tot = buf[p, i, core, sub(u)].astype(F32) + drecv[p, i, sub(u)].astype(F32)
+            for way in range(2):
+                ring_copy(p, way, hch - 1 - way, u, 0).wait_recv()
+                tot = tot + ring[p, way, hch - 1 - way, sub(u)].astype(F32)
+            y_slot(p, chip, core, u)[...] = (xo[p, sub(u)] + tot).astype(BF16)
+            ag_ring(p, 0, 0, u).start()
+            ag_ring(p, 1, 0, u).start()
+            ag_d2d(p, 0, u).start()
+
+    for cp in w1_ld:
+        cp.wait()
+    base_qkv(0)
+    for cp in w2_ld:
+        cp.wait()
+    base_gu(0, 0)
+    mid_service(0, 0)
+    base_gu(0, 1)
+    mid_service(1, 0)
+    mid_service(0, 1)
+    base_qkv(1)
+    mid_service(1, 1)
+    mid_service(0, 2)
+    base_gu(1, 0)
+    mid_service(1, 2)
+    mid_service(0, 3)
+    for cp in c_ld + b_ld + o_ld + bt_ld:
+        cp.wait()
     attend(0)
+    mid_service(1, 3)
+    bt_out.start()
+    bt_d2d.start()
     gated(0)
+    pieces(0, 0, 3)
+    ring_step(0, 0)
+    mid_scatter(0)
+    pieces(0, 3, 8)
+    ring_step(0, 1)
+    base_gu(1, 1)
     bt_out.wait_recv()
     bt_fwd.start()
-    pieces(0, 0, 3)
-    ring_step(0, 0)
-    pieces(0, 3, 8)
     attend(1)
-    ring_step(0, 1)
+    ring_step(0, 2)
     gated(1)
+    mid_gather(0)
     pieces(1, 0, 3)
     ring_step(1, 0)
-    ring_step(0, 2)
+    ring_step(0, 3)
+    mid_scatter(1)
     pieces(1, 3, 8)
     ring_step(1, 1)
-    ring_step(0, 3)
-    ring_step(1, 2)
     bt_d2d.wait_recv()
     bt_fwd.wait_recv()
-    finish_sum(0)
+    lora_out(0)
+    finish_y(0)
+    ring_step(1, 2)
+    mid_gather(1)
+    ag_service(0, 0)
     ring_step(1, 3)
-    finish_y(0)
-    finish_sum(1)
-    ag_service(0, 0)
+    ag_service(0, 1)
+    lora_out(1)
     finish_y(1)
-    ag_service(0, 1)
+    ag_service(0, 2)
     ag_service(1, 0)
-    ag_service(0, 2)
+    ag_service(0, 3)
     ag_service(1, 1)
-    ag_service(0, 3)
     ag_service(1, 2)
-    finish_out(0)
     ag_service(1, 3)
-    finish_out(1)
+    for p in range(PASSES):
+        for u in range(SUBS):
+            for i in range(8):
+                ag_d2d(p, i, u).wait_recv()
 
     for p in range(PASSES):
         for i in range(8):
             mid_d2d(p, i).wait_send()
             d2d(p, i).wait_send()
-            ag_d2d(p, i).wait_send()
+        for d in range(1, hch):
+            mg_copy(p, d).wait_send()
+        for d in range(1, chips):
+            mid_send(p, d).wait_send()
+        mid_part(p).wait_send()
         for way in range(2):
             for s in range(hch - way):
                 mid_ring(p, way, s).wait_send()
-                ring_copy(p, way, s, 0).wait_send()
-                ag_ring(p, way, s).wait_send()
-        for d in range(1, hch):
-            mg_copy(p, d).wait_send()
-        out_copy(p).wait()
+                for u in range(SUBS):
+                    ring_copy(p, way, s, u, 0).wait_send()
+                    ag_ring(p, way, s, u).wait_send()
+        for u in range(SUBS):
+            for i in range(8):
+                ag_d2d(p, i, u).wait_send()
     bt_out.wait_send()
     bt_d2d.wait_send()
     bt_fwd.wait_send()
@@ -468,7 +502,6 @@
         mrows = 2 * rank // (chips // 2)
         share = rank // n
 
-        ids = jnp.repeat(adapter_ids, seq).reshape(1, tokens)
         hd = head // 2
         inv_freq = ROPE_BASE ** (-np.arange(hd, dtype=np.float32) / np.float32(hd))
         ang = inv_freq[:, None] * np.arange(seq, dtype=np.float32)[None, :]
@@ -484,7 +517,7 @@
         def bt(b):
             return b.transpose(0, 2, 3, 1).reshape(n_adapt, wide, rank)
 
-        args = (x_blk.reshape(tokens, d_model), ids, norm_gain.reshape(1, d_model), cos_t, sin_t,
+        args = (x_blk.reshape(tokens, d_model), adapter_ids, norm_gain.reshape(d_model // 128, 128), cos_t, sin_t,
                 wt(w_query), wt(w_key), wt(w_value), w_out.reshape(wide, d_model), w_gate, w_up, w_down,
                 at(a_query), at(a_key), at(a_value), at(a_gate), at(a_up),
                 bt(b_query), bt(b_key), bt(b_value), b_gate.reshape(n_adapt * rank, ff), b_up.reshape(n_adapt * rank, ff),
@@ -494,6 +527,12 @@
         dma = pltpu.SemaphoreType.DMA
         cfg = (n, tokens, seq, n_adapt, rank, heads, head, ff)
         scratch = [
+            pltpu.SMEM((seqs,), jnp.int32),
+            pltpu.VMEM((1, tokens), jnp.int32),
+            pltpu.VMEM((d_model // 128, 128), F32),
+            pltpu.VMEM((1, d_model), F32),
+            pltpu.VMEM((hd, half), F32),
+            pltpu.VMEM((hd, half), F32),
             pltpu.VMEM((tokens, d_model), BF16),
             pltpu.VMEM((tokens, d_model), BF16),
             pltpu.VMEM((5 * n_adapt * share, d_model), BF16),
@@ -513,28 +552,30 @@
             pltpu.VMEM((3 * wide, half), BF16),
             pltpu.VMEM((wide, tokens), BF16),
             pltpu.VMEM((tokens, ff), BF16),
-            pltpu.VMEM((PASSES, 2 * rank, half), BF16),
-            pltpu.VMEM((PASSES, chips, 2, rows + 16, cols), BF16),
-            pltpu.VMEM((PASSES, chips, rows + 16, cols), BF16),
-            pltpu.VMEM((PASSES, 2, chips // 2, rows + 16, cols), BF16),
+            pltpu.VMEM((PASSES, 2, 2, 2 * rank, rows), BF16),
+            pltpu.VMEM((PASSES, 2, 2 * rank, rows), BF16),
+            pltpu.VMEM((PASSES, chips - 1, mrows, rows), BF16),
+            pltpu.VMEM((PASSES, chips, 2, rows, cols), BF16),
+            pltpu.VMEM((PASSES, chips, rows, cols), BF16),
+            pltpu.VMEM((PASSES, 2, chips // 2, rows, cols), BF16),
             pltpu.VMEM((PASSES, chips // 2, mrows, rows), BF16),
             pltpu.VMEM((PASSES, rows, cols), F32),
-            pltpu.VMEM((tokens, d_model), BF16),
-            dma((48,)),
+            dma((56,)),
             dma((PASSES, 2, 4)), dma((PASSES, 2, 4)), dma((PASSES, 8)), dma((PASSES, 8)),
             dma((3,)), dma((3,)), dma((PASSES, 8)), dma((PASSES, 8)),
-            dma((PASSES, 2, 4)), dma((PASSES, 2, 4)), dma((PASSES, 3)), dma((PASSES, 3)),
-            dma((PASSES, 2, 4)), dma((PASSES, 2, 4)), dma((PASSES, 8)), dma((PASSES, 8)),
-            dma((PASSES,)),
+            dma((PASSES, 2, 4, SUBS)), dma((PASSES, 2, 4, SUBS)),
+            dma((PASSES,)), dma((PASSES,)), dma((PASSES, chips - 1)), dma((PASSES, chips - 1)),
+            dma((PASSES, 3)), dma((PASSES, 3)),
+            dma((PASSES, 2, 4, SUBS)), dma((PASSES, 2, 4, SUBS)), dma((PASSES, 8, SUBS)), dma((PASSES, 8, SUBS)),
         ]
         y = pl.pallas_call(
             functools.partial(layer_kernel, cfg),
-            out_shape=jax.ShapeDtypeStruct((tokens, d_model), BF16),
-            in_specs=[hbm] + [vmem] * 4 + [hbm] * 21,
-            out_specs=hbm,
+            out_shape=pltpu.VMEM((tokens, d_model), BF16),
+            in_specs=[hbm] * 26,
+            out_specs=vmem,
             scratch_shapes=scratch,
             compiler_params=pltpu.CompilerParams(collective_id=0, has_side_effects=True,
-                                                 vmem_limit_bytes=67_000_000),
+                                                 vmem_limit_bytes=59_000_000),
         )(*args)
         return y.reshape(x_blk.shape)
 

time: 118 us -> 109 us (0.924)
  local copies, waits for them, and re-layouts: 8.09 us -> 2.36 us
  Pallas kernels: 110 us -> 107 us
    unnamed x1, local copies, waits for them, and re-layouts: 5.39 us -> 2.36 us
    pallas_call x1, Pallas kernels: 110 us -> 107 us  [local_layer(): pl.pallas_call(functools.partial(layer_kernel, cfg), out_shape=pltpu.VMEM...]
    reshape x1 -> x0, local copies, waits for them, and re-layouts: 1.31 us -> none  [local_layer(): norm_gain.reshape(1, d_model)]
where the time goes in v2:
time: 109 us
  Pallas kernels  107 us (98%)
  local copies, waits for them, and re-layouts  2.36 us (2%)
    pallas_call x1, Pallas kernels, local_layer(): pl.pallas_call(functools.partial(layer_kernel, cfg), out_shape=pltpu.VMEM...  107 us
    unnamed x1, local copies, waits for them, and re-layouts  2.36 us

profile of v2, /device:TPU:21, one launch (start us, length us, event | category | flops | bytes accessed | tf_op | source)
XLA Modules:
  0.0 109.0 jit_solution(5474187540781385762)
XLA Ops:
  0.0 106.7 %shard_map.244 = bf16[1024,2560]{1,0:T(8,128)(2,1)S(1)} custom-call(bf16[1024,2560]{1,0:T(8,128)(2,1)} %bitcast.43, s32[32]{0:T(128)} %ids_hbm.1, f32[20,128]{1,0:T(8,128)} %bitcast.61, f32[40,512]{1,0:T(8,128)} %constant.4.clone.cos_hbm, f32[40,512]{1,0:T(8,128)} %constant.5.clone.sin_hbm, bf16[160,2560]{1,0:T(8,128)(2,1)} %bitcast.44, ...), custom_call_target="tpu_custom_call" | custom-call | tf_op jit(solution)/shard_map/pallas_call | solution.py:571
  106.7 2.4 %copy.28 = bf16[32,32,2560]{2,1,0:T(8,128)(2,1)} copy(bf16[32,32,2560]{2,1,0:T(8,128)(2,1)S(1)} %bitcast.42) | data formatting | bytes 10485760

commit v3 on v2

--- a/solution.py
+++ b/solution.py
@@ -30,7 +30,7 @@
                  ids_s, ids_ref, gain_v, gain_ref, cos_ref, sin_ref, xv, hv, a_v, wqkv, wgu, bqkv, bgu, wo_v, wd_v, ao_v, ad_v, btg,
                  qkv_base, gu_base, gm, mmk, qk_v, ot_v, m_v, midp, midr, midx,
                  buf, drecv, ring, mg, xo,
-                 ld, mid_s, mid_r, md_s, md_r, bt_s, bt_r, dd_s, dd_r, rg_s, rg_r,
+                 ld, mf_s, mf_r, mid_s, mid_r, md_s, md_r, bt_s, bt_r, dd_s, dd_r, rg_s, rg_r,
                  mp_s, mp_r, mx_s, mx_r, mg_s, mg_r, ag_s, ag_r, ad_s, ad_r):
     n, tokens, seq, n_adapt, rank, heads, head, ff = cfg
     chips = n // 2
@@ -58,29 +58,41 @@
         return pltpu.make_async_remote_copy(src_ref=src, dst_ref=dst, send_sem=ssem, recv_sem=rsem,
                                             device_id={'tensor': to}, device_id_type=MESH)
 
-    loads = []
-
-    def load(src, dst):
-        cp = pltpu.make_async_copy(src, dst, ld.at[len(loads)])
-        cp.start()
-        loads.append(cp)
-        return cp
+    def drain_recv(ref, sem):
+        rcopy(ref, ref, sem, sem, partner).wait_recv()
+
+    def drain_send(ref, sem):
+        rcopy(ref, ref, sem, sem, partner).wait_send()
+
+    used = []
+
+    def load(buffer, *pairs):
+        sem = ld.at[len(used)]
+        used.append(sem)
+        for src, dst in pairs:
+            pltpu.make_async_copy(src, dst, sem).start()
+        return pltpu.make_async_copy(buffer, buffer, sem)
 
     tile = tokens // 4
-    g_ld = [load(ids_hbm, ids_s), load(gain_hbm, gain_v)]
-    x_ld = [load(x_hbm.at[pl.ds(i * tile, tile)], xv.at[pl.ds(i * tile, tile)]) for i in range(4)]
-    a_ld = [load(src, a_v.at[pl.ds(i * n_adapt * share, n_adapt * share)]) for i, src in enumerate((aq, ak, av, ag, au))]
+    ids_ld = load(ids_s, (ids_hbm, ids_s))
+    gain_ld = load(gain_v, (gain_hbm, gain_v))
+    x_ld = [load(xv.at[pl.ds(i * tile, tile)], (x_hbm.at[pl.ds(i * tile, tile)], xv.at[pl.ds(i * tile, tile)])) for i in range(4)]
+    a_rows = n_adapt * share
+    a_ld = load(a_v, *((src, a_v.at[pl.ds(i * a_rows, a_rows)]) for i, src in enumerate((aq, ak, av, ag, au))))
 
     barrier = pltpu.get_barrier_semaphore()
     for step in range(1, n):
         pl.semaphore_signal(barrier, inc=1, device_id={'tensor': lax.rem(me + step, n)}, device_id_type=MESH)
 
-    w1_ld = [load(src, wqkv.at[pl.ds(i * wide, wide)]) for i, src in enumerate((wq, wk, wv))]
-    w2_ld = [load(src, wgu.at[:, pl.ds(i * ff, ff)]) for i, src in enumerate((wg, wu))]
-
-    c_ld = [load(cos_hbm, cos_ref), load(sin_hbm, sin_ref)]
-    for cp in g_ld:
-        cp.wait()
+    w1_ld = load(wqkv, *((src, wqkv.at[pl.ds(i * wide, wide)]) for i, src in enumerate((wq, wk, wv))))
+    bt_rows = pl.ds(pl.multiple_of(lax.rem(me, 4) * wide, 16), wide)
+    bt_ld = load(btg.at[bt_rows], *((src.at[a], btg.at[bt_rows, pl.ds((st * n_adapt + a) * rank, rank)])
+                                    for st, src in enumerate((bo, bd)) for a in range(n_adapt)))
+    w2_ld = load(wgu, *((src, wgu.at[:, pl.ds(i * ff, ff)]) for i, src in enumerate((wg, wu))))
+    cos_ld = load(cos_ref, (cos_hbm, cos_ref))
+    sin_ld = load(sin_ref, (sin_hbm, sin_ref))
+    ids_ld.wait()
+    gain_ld.wait()
     where_seq = lax.broadcasted_iota(jnp.int32, (1, tokens), 1) // seq
     ids_all = jnp.zeros((1, tokens), jnp.int32)
     for b in range(tokens // seq):
@@ -89,19 +101,17 @@
     gain_ref[...] = jnp.concatenate([gain_v[b:b + 1, :] for b in range(gain_v.shape[0])], axis=1)
 
     nt = 128
-    for i in range(4):
+
+    def norm_tiles(i):
         x_ld[i].wait()
 
-        def norm_tile(j, carry, i=i):
+        def body(j, carry):
             r = pl.ds(pl.multiple_of(i * tile + j * nt, nt), nt)
             xf = xv[r, :].astype(F32)
             inv = lax.rsqrt(jnp.mean(xf * xf, axis=-1, keepdims=True) + EPS)
             hv[r, :] = (xf * inv * gain_ref[...]).astype(BF16)
             return carry
-        lax.fori_loop(0, tile // nt, norm_tile, 0)
-
-    for cp in a_ld:
-        cp.wait()
+        lax.fori_loop(0, tile // nt, body, 0)
 
     def mid_slot(hf, c, k):
         return gm.at[hf, 2 * wrap(c) + k]
@@ -109,7 +119,7 @@
     def mid_ring(hf, way, s):
         sg = sign if way == 0 else -sign
         slot = mid_slot(hf, chip - sg * s, core)
-        return rcopy(slot, slot, mid_s.at[hf, way, s], mid_r.at[hf, way, s], dev(chip + sg))
+        return rcopy(slot, slot, mid_s.at[0], mid_r.at[way, s], dev(chip + sg))
 
     def mid_d2d(hf, i):
         if i == 0:
@@ -119,7 +129,15 @@
         else:
             c = chip + sign * (i - 4)
         slot = mid_slot(hf, c, core)
-        return rcopy(slot, slot, md_s.at[hf, i], md_r.at[hf, i], partner)
+        return rcopy(slot, slot, md_s.at[hf], md_r.at[hf], partner)
+
+    def mid_direct(d):
+        return rcopy(gm.at[0, me], gm.at[0, me], mf_s.at[0], mf_r.at[0], dev(chip + d))
+
+    def mid_forward():
+        drain_recv(gm.at[0, pl.ds(0, chips - 1)], mf_r.at[0])
+        for i in range(1, 8):
+            mid_d2d(0, i).start()
 
     hch = chips // 2
 
@@ -135,7 +153,7 @@
     def ids_of(start, size):
         return ids_ref[:, pl.ds(start, size)]
 
-    for hf in range(PASSES):
+    def rank_part(hf):
         mids = mm(a_v[...], hv[pl.ds(hf * half, half), :], 1, 1)
         ids = ids_of(hf * half, half)
         out = []
@@ -144,57 +162,68 @@
             for a in range(n_adapt):
                 lo = (st * n_adapt + a) * share
                 acc = jnp.where(ids == a, mids[lo:lo + share], acc)
-            out.append(acc)
-        out.append(jnp.zeros((share, half), F32))
+            out += [acc[:, :half // 2], acc[:, half // 2:]]
         gm[hf, me] = jnp.concatenate(out, axis=0).astype(BF16)
         if hf == 0:
             pl.semaphore_wait(barrier, n - 1)
-        mid_ring(hf, 0, 0).start()
-        mid_ring(hf, 1, 0).start()
+            for d in (4, 3, 5, 2, 6, 1, 7):
+                mid_direct(d).start()
+        else:
+            mid_ring(hf, 0, 0).start()
+            mid_ring(hf, 1, 0).start()
         mid_d2d(hf, 0).start()
 
-    b_ld = []
-    for i, src in enumerate((bq, bk, bv)):
-        for a in range(n_adapt):
-            b_ld.append(load(src.at[a], bqkv.at[pl.ds(i * wide, wide), pl.ds(a * rank, rank)]))
-    b_ld += [load(src, bgu.at[:, pl.ds(i * ff, ff)]) for i, src in enumerate((bg, bu))]
-    o_ld = [load(wo, wo_v), load(wd, wd_v)]
-    for a in range(n_adapt):
-        o_ld.append(load(ao.at[a], ao_v.at[:, pl.ds(a * rank, rank)]))
-        o_ld.append(load(ad.at[a], ad_v.at[:, pl.ds(a * rank, rank)]))
-    bt_rows = pl.ds(pl.multiple_of(lax.rem(me, 4) * wide, 16), wide)
-    bt_ld = []
-    for st, src in enumerate((bo, bd)):
-        for a in range(n_adapt):
-            bt_ld.append(load(src.at[a], btg.at[bt_rows, pl.ds((st * n_adapt + a) * rank, rank)]))
-
+    norm_tiles(0)
+    norm_tiles(1)
+    a_ld.wait()
+    rank_part(0)
+    norm_tiles(2)
+    norm_tiles(3)
+    rank_part(1)
+
+    late = [
+        load(bqkv, *((src.at[a], bqkv.at[pl.ds(i * wide, wide), pl.ds(a * rank, rank)])
+                     for i, src in enumerate((bq, bk, bv)) for a in range(n_adapt))),
+        load(bgu, *((src, bgu.at[:, pl.ds(i * ff, ff)]) for i, src in enumerate((bg, bu)))),
+        load(wo_v, (wo, wo_v)),
+        load(wd_v, (wd, wd_v)),
+        load(ao_v, *((ao.at[a], ao_v.at[:, pl.ds(a * rank, rank)]) for a in range(n_adapt))),
+        load(ad_v, *((ad.at[a], ad_v.at[:, pl.ds(a * rank, rank)]) for a in range(n_adapt))),
+    ]
     def base_qkv(hf):
         r = pl.ds(hf * half, half)
         qkv_base[:, r] = mm(wqkv[...], hv[r, :], 1, 1)
 
-    def base_gu(hf, part):
+    def base_gu(hf):
         r = pl.ds(hf * half, half)
-        c = pl.ds(part * ff, ff)
-        gu_base[r, c] = mm(hv[r, :], wgu[:, c])
+        gu_base[r, :] = mm(hv[r, :], wgu[...])
 
     pair = chip + 1 - 2 * lax.rem(chip, 2)
 
     def bt_slot(dv):
         return btg.at[pl.ds(pl.multiple_of(lax.rem(dv, 4) * wide, 16), wide)]
 
-    bt_out = rcopy(bt_slot(me), bt_slot(me), bt_s.at[0], bt_r.at[0], dev(pair))
-    bt_d2d = rcopy(bt_slot(me), bt_slot(me), bt_s.at[1], bt_r.at[1], partner)
-    bt_fwd = rcopy(bt_slot(dev(pair)), bt_slot(dev(pair)), bt_s.at[2], bt_r.at[2], partner)
+    bt_half = n_adapt * rank
+
+    def bt_out(st):
+        slot = btg.at[pl.ds(pl.multiple_of(lax.rem(me, 4) * wide, 16), wide), pl.ds(st * bt_half, bt_half)]
+        return rcopy(slot, slot, bt_s.at[0], bt_r.at[0], dev(pair))
+
+    bt_d2d = rcopy(bt_slot(me), bt_slot(me), bt_s.at[0], bt_r.at[1], partner)
+    bt_fwd = rcopy(bt_slot(dev(pair)), bt_slot(dev(pair)), bt_s.at[0], bt_r.at[2], partner)
     def build_mask(hf, st):
         ids = ids_of(hf * half, half)
-        parts = [gm[hf, t].astype(F32)[st * share:(st + 1) * share] for t in range(n)]
-        full = jnp.concatenate(parts, axis=0)
+        lo, hi = [], []
+        for t in range(n):
+            blk = gm[hf, t].astype(F32)
+            lo.append(blk[2 * st * share:(2 * st + 1) * share])
+            hi.append(blk[(2 * st + 1) * share:(2 * st + 2) * share])
+        full = jnp.concatenate([jnp.concatenate(lo, axis=0), jnp.concatenate(hi, axis=0)], axis=1)
         for a in range(n_adapt):
             mmk[pl.ds(a * rank, rank), :] = jnp.where(ids == a, full, 0.0).astype(BF16)
 
     def attend(hf):
-        for i in range(8):
-            mid_d2d(hf, i).wait_recv()
+        drain_recv(gm.at[hf, pl.ds(0, chips)], md_r.at[hf])
         r = pl.ds(hf * half, half)
         hd = head // 2
         for st in range(3):
@@ -255,7 +284,7 @@
         return midp.at[p, core, lax.rem(c, 2), pl.ds(pl.multiple_of((c // 2) * mrows, mrows), mrows)]
 
     def mid_send(p, d):
-        return rcopy(mid_block(p, chip + d), midx.at[p, d - 1], mx_s.at[p, d - 1], mx_r.at[p, d - 1], dev(chip + d))
+        return rcopy(mid_block(p, chip + d), midx.at[p, d - 1], mx_s.at[p], mx_r.at[p], dev(chip + d))
 
     def mid_scatter(p):
         mid_part(p).wait_recv()
@@ -265,69 +294,64 @@
 
     def mid_gather(p):
         tot = mid_block(p, chip)[...].astype(F32)
+        drain_recv(midx.at[p], mx_r.at[p])
         for d in range(1, chips):
-            mid_send(p, d).wait_recv()
             tot = tot + midx[p, d - 1].astype(F32)
         mg[p, chip // 2] = tot.astype(BF16)
         for d in range(1, hch):
             mg_copy(p, d).start()
 
-    def offset_of(i):
-        mag = hch - (i + 1) // 2
-        return mag * (2 * lax.rem(jnp.int32(i), 2) - 1)
-
-    def d2d(p, i):
-        return rcopy(buf.at[p, i, 1 - core], drecv.at[p, i], dd_s.at[p, i], dd_r.at[p, i], partner)
-
-    def piece(p, i):
-        e = wrap(chip + offset_of(i))
-        odd = lax.rem(e, 2)
-        grp = e // 2
-        r0 = pl.multiple_of(p * half + odd * 2 * rows, 2 * rows)
-        c = pl.ds(pl.multiple_of(grp * cols, 128), cols)
-        val = mm(m_v[pl.ds(r0, 2 * rows), :], wd_v[:, c]) + mm(ot_v[:, pl.ds(r0, 2 * rows)], wo_v[:, c], 0, 0)
-        for k in range(2):
-            buf[p, i, k] = val[k * rows:(k + 1) * rows].astype(BF16)
-        d2d(p, i).start()
-
-    def pieces(p, lo, hi):
-        def body(i, carry):
-            piece(p, i)
+    def d2d(p, e):
+        return rcopy(buf.at[p, e, 1 - core], drecv.at[p, e], dd_s.at[p], dd_r.at[p, e], partner)
+
+    def group(p, g):
+        c = pl.ds(pl.multiple_of(g * cols, 128), cols)
+        r = pl.ds(p * half, half)
+        val = mm(m_v[r, :], wd_v[:, c]) + mm(ot_v[:, r], wo_v[:, c], 0, 0)
+        for q in range(4):
+            buf[p, 2 * g + q // 2, q % 2] = val[q * rows:(q + 1) * rows].astype(BF16)
+        d2d(p, 2 * g).start()
+        d2d(p, 2 * g + 1).start()
+
+    def groups(p, lo, hi):
+        parity = lax.rem(chip, 2)
+        own = chip // 2
+
+        def body(t, carry):
+            near = jnp.where(t == 1, 1 - 2 * parity, 2 * parity - 1)
+            off = jnp.where(t == 0, 2, jnp.where(t == 3, 0, near))
+            group(p, lax.rem(own + off + 4, 4))
             return carry
         lax.fori_loop(lo, hi, body, 0)
 
     def sub(u):
         return pl.ds(u * (rows // SUBS), rows // SUBS)
 
-    def ring_copy(p, way, s, u, i):
+    def ring_dest(way, s):
+        return wrap(chip + sign * (hch - s)) if way == 0 else wrap(chip - sign * (hch - 1 - s))
+
+    def ring_copy(p, way, s, u):
         sg = sign if way == 0 else -sign
-        return rcopy(buf.at[p, i, core, sub(u)], ring.at[p, way, s, sub(u)],
-                     rg_s.at[p, way, s, u], rg_r.at[p, way, s, u], dev(chip + sg))
-
-    def ring_index(way, s):
-        if way == 0:
-            return 0 if s == 0 else 2 * s - 1 + core
-        return 2 * s + 2 - core
-
-    def ring_step(p, s):
-        for u in range(SUBS):
-            for way in range(2):
-                last = hch - way
-                if s >= last:
-                    continue
-                i = ring_index(way, s)
-                if u == 0:
-                    d2d(p, i).wait_recv()
-                tot = buf[p, i, core, sub(u)].astype(F32) + drecv[p, i, sub(u)].astype(F32)
-                if s > 0:
-                    ring_copy(p, way, s - 1, u, 0).wait_recv()
-                    tot = tot + ring[p, way, s - 1, sub(u)].astype(F32)
-                buf[p, i, core, sub(u)] = tot.astype(BF16)
-                ring_copy(p, way, s, u, i).start()
+        return rcopy(buf.at[p, ring_dest(way, s), core, sub(u)], ring.at[p, way, s, sub(u)],
+                     rg_s.at[p], rg_r.at[p, way, s, u], dev(chip + sg))
+
+    met = set()
+
+    def ring_part(p, way, s, u):
+        e = ring_dest(way, s)
+        if (p, way, s) not in met:
+            met.add((p, way, s))
+            d2d(p, e).wait_recv()
+        tot = buf[p, e, core, sub(u)].astype(F32) + drecv[p, e, sub(u)].astype(F32)
+        if s > 0:
+            ring_copy(p, way, s - 1, u).wait_recv()
+            tot = tot + ring[p, way, s - 1, sub(u)].astype(F32)
+        buf[p, e, core, sub(u)] = tot.astype(BF16)
+        ring_copy(p, way, s, u).start()
 
     def mg_copy(p, d):
         slot = mg.at[p, chip // 2]
-        return rcopy(slot, slot, mg_s.at[p, d - 1], mg_r.at[p, d - 1], dev(chip + 2 * d))
+        return rcopy(slot, slot, mg_s.at[p], mg_r.at[p], dev(chip + 2 * d))
 
     def y_rows(p, c, k, u):
         c = wrap(c)
@@ -342,7 +366,7 @@
     def ag_ring(p, way, s, u):
         sg = sign if way == 0 else -sign
         slot = y_slot(p, chip - sg * s, core, u)
-        return rcopy(slot, slot, ag_s.at[p, way, s, u], ag_r.at[p, way, s, u], dev(chip + sg))
+        return rcopy(slot, slot, ag_s.at[p], ag_r.at[p, way, s, u], dev(chip + sg))
 
     def ag_d2d(p, i, u):
         if i == 0:
@@ -352,21 +376,16 @@
         else:
             c = chip + sign * (i - 4)
         slot = y_slot(p, c, core, u)
-        return rcopy(slot, slot, ad_s.at[p, i, u], ad_r.at[p, i, u], partner)
-
-    def ag_service(p, s):
-        for u in range(SUBS):
-            for way in range(2):
-                last = hch - way
-                if s < last:
-                    ag_ring(p, way, s, u).wait_recv()
-                    if s + 1 < last:
-                        ag_ring(p, way, s + 1, u).start()
-                    ag_d2d(p, (1 if way == 0 else 5) + s, u).start()
+        return rcopy(slot, slot, ad_s.at[p], ad_r.at[p], partner)
+
+    def ag_part(p, way, s, u):
+        ag_ring(p, way, s, u).wait_recv()
+        if s + 1 < hch - way:
+            ag_ring(p, way, s + 1, u).start()
+        ag_d2d(p, (1 if way == 0 else 5) + s, u).start()
 
     def lora_out(p):
-        for d in range(1, hch):
-            mg_copy(p, d).wait_recv()
+        drain_recv(midx.at[p, pl.ds(0, hch - 1)], mg_r.at[p])
         ids = ids_of(y_rows(p, chip, core, 0), rows)
         mids = jnp.concatenate([mg[p, g].astype(F32) for g in range(hch)], axis=0)
         parts = []
@@ -377,103 +396,146 @@
         r = pl.ds(y_rows(p, chip, core, 0), rows)
         xo[p] = xv[r, y_cols(chip)].astype(F32) + scale * lora
 
-    def finish_y(p):
-        i = 2 * hch - 1
-        d2d(p, i).wait_recv()
-        for u in range(SUBS):
-            tot = buf[p, i, core, sub(u)].astype(F32) + drecv[p, i, sub(u)].astype(F32)
-            for way in range(2):
-                ring_copy(p, way, hch - 1 - way, u, 0).wait_recv()
-                tot = tot + ring[p, way, hch - 1 - way, sub(u)].astype(F32)
-            y_slot(p, chip, core, u)[...] = (xo[p, sub(u)] + tot).astype(BF16)
-            ag_ring(p, 0, 0, u).start()
-            ag_ring(p, 1, 0, u).start()
-            ag_d2d(p, 0, u).start()
-
-    for cp in w1_ld:
-        cp.wait()
+    def finish_part(p, u):
+        if (p, 2, 0) not in met:
+            met.add((p, 2, 0))
+            d2d(p, chip).wait_recv()
+        tot = buf[p, chip, core, sub(u)].astype(F32) + drecv[p, chip, sub(u)].astype(F32)
+        for way in range(2):
+            ring_copy(p, way, hch - 1 - way, u).wait_recv()
+            tot = tot + ring[p, way, hch - 1 - way, sub(u)].astype(F32)
+        y_slot(p, chip, core, u)[...] = (xo[p, sub(u)] + tot).astype(BF16)
+        ag_ring(p, 0, 0, u).start()
+        ag_ring(p, 1, 0, u).start()
+        ag_d2d(p, 0, u).start()
+
+    def bt_forward():
+        drain_recv(btg.at[pl.ds(0, wide)], bt_r.at[0])
+        bt_fwd.start()
+
+    def bt_arrived():
+        bt_d2d.wait_recv()
+        bt_fwd.wait_recv()
+
+    def rank_sends_done():
+        drain_send(gm.at[0, pl.ds(0, chips - 1)], mf_s.at[0])
+        drain_send(gm.at[0, pl.ds(0, chips - 1)], mid_s.at[0])
+        for p in range(PASSES):
+            drain_send(gm.at[p, pl.ds(0, chips)], md_s.at[p])
+        drain_send(btg.at[pl.ds(0, 3 * wide)], bt_s.at[0])
+
+    def sum_sends_done(p):
+        drain_send(drecv.at[p], dd_s.at[p])
+        drain_send(midx.at[p, pl.ds(0, hch - 1)], mg_s.at[p])
+        drain_send(midx.at[p], mx_s.at[p])
+        mid_part(p).wait_send()
+        drain_send(drecv.at[p, pl.ds(0, chips - 1)], rg_s.at[p])
+
+    def y_sends_done(p):
+        drain_send(drecv.at[p, pl.ds(0, chips - 1)], ag_s.at[p])
+        drain_send(drecv.at[p], ad_s.at[p])
+
+    def y_arrived(p):
+        drain_recv(drecv.at[p], ad_r.at[p])
+
+    w1_ld.wait()
     base_qkv(0)
-    for cp in w2_ld:
-        cp.wait()
-    base_gu(0, 0)
-    mid_service(0, 0)
-    base_gu(0, 1)
+    bt_ld.wait()
+    bt_out(0).start()
+    bt_d2d.start()
+    w2_ld.wait()
+    base_gu(0)
+    bt_out(1).start()
+    base_qkv(1)
+    mid_forward()
     mid_service(1, 0)
-    mid_service(0, 1)
-    base_qkv(1)
-    mid_service(1, 1)
-    mid_service(0, 2)
-    base_gu(1, 0)
-    mid_service(1, 2)
-    mid_service(0, 3)
-    for cp in c_ld + b_ld + o_ld + bt_ld:
+    for cp in [cos_ld, sin_ld] + late:
         cp.wait()
     attend(0)
+    gated(0)
+    groups(0, 0, 2)
+    mid_service(1, 1)
+    mid_scatter(0)
+    bt_forward()
+    groups(0, 2, 4)
+    ring_part(0, 0, 0, 0)
+    ring_part(0, 1, 0, 0)
+    ring_part(0, 0, 0, 1)
+    ring_part(0, 1, 0, 1)
+    base_gu(1)
+    mid_service(1, 2)
+    ring_part(0, 1, 1, 0)
+    ring_part(0, 0, 1, 0)
+    ring_part(0, 1, 1, 1)
+    mid_gather(0)
+    ring_part(0, 0, 1, 1)
     mid_service(1, 3)
-    bt_out.start()
-    bt_d2d.start()
-    gated(0)
-    pieces(0, 0, 3)
-    ring_step(0, 0)
-    mid_scatter(0)
-    pieces(0, 3, 8)
-    ring_step(0, 1)
-    base_gu(1, 1)
-    bt_out.wait_recv()
-    bt_fwd.start()
     attend(1)
-    ring_step(0, 2)
+    ring_part(0, 0, 2, 0)
+    ring_part(0, 1, 2, 0)
     gated(1)
-    mid_gather(0)
-    pieces(1, 0, 3)
-    ring_step(1, 0)
-    ring_step(0, 3)
     mid_scatter(1)
-    pieces(1, 3, 8)
-    ring_step(1, 1)
-    bt_d2d.wait_recv()
-    bt_fwd.wait_recv()
+    groups(1, 0, 2)
+    bt_arrived()
     lora_out(0)
-    finish_y(0)
-    ring_step(1, 2)
+    ring_part(0, 0, 2, 1)
+    ring_part(0, 1, 2, 1)
+    ring_part(0, 0, 3, 0)
+    groups(1, 2, 4)
+    ring_part(1, 0, 0, 1)
+    ring_part(1, 0, 0, 0)
+    ring_part(1, 1, 0, 0)
+    ring_part(1, 1, 0, 1)
+    ring_part(0, 0, 3, 1)
     mid_gather(1)
-    ag_service(0, 0)
-    ring_step(1, 3)
-    ag_service(0, 1)
+    finish_part(0, 0)
+    ring_part(1, 1, 1, 0)
+    ring_part(1, 0, 1, 1)
+    ring_part(1, 1, 1, 1)
+    ring_part(1, 0, 1, 0)
+    finish_part(0, 1)
+    ag_part(0, 1, 0, 0)
+    ring_part(1, 1, 2, 0)
+    ag_part(0, 0, 0, 0)
     lora_out(1)
-    finish_y(1)
-    ag_service(0, 2)
-    ag_service(1, 0)
-    ag_service(0, 3)
-    ag_service(1, 1)
-    ag_service(1, 2)
-    ag_service(1, 3)
+    ring_part(1, 1, 2, 1)
+    ring_part(1, 0, 2, 1)
+    ag_part(0, 1, 0, 1)
+    ring_part(1, 0, 2, 0)
+    ag_part(0, 1, 1, 0)
+    ag_part(0, 0, 0, 1)
+    ag_part(0, 0, 1, 0)
+    ring_part(1, 0, 3, 1)
+    ag_part(0, 1, 1, 1)
+    ring_part(1, 0, 3, 0)
+    ag_part(0, 1, 2, 0)
+    ag_part(0, 0, 1, 1)
+    ag_part(0, 0, 2, 0)
+    ag_part(0, 1, 2, 1)
+    finish_part(1, 1)
+    finish_part(1, 0)
+    ag_part(0, 0, 2, 1)
+    ag_part(0, 0, 3, 0)
+    ag_part(1, 1, 0, 1)
+    ag_part(1, 0, 0, 1)
+    ag_part(1, 1, 0, 0)
+    ag_part(1, 0, 0, 0)
+    ag_part(0, 0, 3, 1)
+    ag_part(1, 1, 1, 1)
+    ag_part(1, 0, 1, 1)
+    ag_part(1, 1, 1, 0)
+    ag_part(1, 0, 1, 0)
+    ag_part(1, 1, 2, 1)
+    ag_part(1, 0, 2, 1)
+    ag_part(1, 1, 2, 0)
+    ag_part(1, 0, 2, 0)
+    ag_part(1, 0, 3, 1)
+    ag_part(1, 0, 3, 0)
+    rank_sends_done()
     for p in range(PASSES):
-        for u in range(SUBS):
-            for i in range(8):
-                ag_d2d(p, i, u).wait_recv()
-
-    for p in range(PASSES):
-        for i in range(8):
-            mid_d2d(p, i).wait_send()
-            d2d(p, i).wait_send()
-        for d in range(1, hch):
-            mg_copy(p, d).wait_send()
-        for d in range(1, chips):
-            mid_send(p, d).wait_send()
-        mid_part(p).wait_send()
-        for way in range(2):
-            for s in range(hch - way):
-                mid_ring(p, way, s).wait_send()
-                for u in range(SUBS):
-                    ring_copy(p, way, s, u, 0).wait_send()
-                    ag_ring(p, way, s, u).wait_send()
-        for u in range(SUBS):
-            for i in range(8):
-                ag_d2d(p, i, u).wait_send()
-    bt_out.wait_send()
-    bt_d2d.wait_send()
-    bt_fwd.wait_send()
+        sum_sends_done(p)
+        y_arrived(p)
+        y_sends_done(p)
 
 
 def solution(mesh):
@@ -547,7 +609,7 @@
             pltpu.VMEM((4 * wide, 2 * n_adapt * rank), BF16),
             pltpu.VMEM((3 * wide, tokens), F32),
             pltpu.VMEM((tokens, 2 * ff), F32),
-            pltpu.VMEM((PASSES, n, 6 * share, half), BF16),
+            pltpu.VMEM((PASSES, n, 10 * share, half // 2), BF16),
             pltpu.VMEM((n_adapt * rank, half), BF16),
             pltpu.VMEM((3 * wide, half), BF16),
             pltpu.VMEM((wide, tokens), BF16),
@@ -560,13 +622,13 @@
             pltpu.VMEM((PASSES, 2, chips // 2, rows, cols), BF16),
             pltpu.VMEM((PASSES, chips // 2, mrows, rows), BF16),
             pltpu.VMEM((PASSES, rows, cols), F32),
-            dma((56,)),
-            dma((PASSES, 2, 4)), dma((PASSES, 2, 4)), dma((PASSES, 8)), dma((PASSES, 8)),
-            dma((3,)), dma((3,)), dma((PASSES, 8)), dma((PASSES, 8)),
-            dma((PASSES, 2, 4, SUBS)), dma((PASSES, 2, 4, SUBS)),
-            dma((PASSES,)), dma((PASSES,)), dma((PASSES, chips - 1)), dma((PASSES, chips - 1)),
-            dma((PASSES, 3)), dma((PASSES, 3)),
-            dma((PASSES, 2, 4, SUBS)), dma((PASSES, 2, 4, SUBS)), dma((PASSES, 8, SUBS)), dma((PASSES, 8, SUBS)),
+            dma((18,)), dma((1,)), dma((1,)),
+            dma((1,)), dma((2, 4)), dma((PASSES,)), dma((PASSES,)),
+            dma((1,)), dma((3,)), dma((PASSES,)), dma((PASSES, chips)),
+            dma((PASSES,)), dma((PASSES, 2, 4, SUBS)),
+            dma((PASSES,)), dma((PASSES,)), dma((PASSES,)), dma((PASSES,)),
+            dma((PASSES,)), dma((PASSES,)),
+            dma((PASSES,)), dma((PASSES, 2, 4, SUBS)), dma((PASSES,)), dma((PASSES,)),
         ]
         y = pl.pallas_call(
             functools.partial(layer_kernel, cfg),

time: 109 us -> 101 us (0.927)
  Pallas kernels: 107 us -> 98.8 us
    pallas_call x1, Pallas kernels: 107 us -> 98.8 us  [local_layer(): pl.pallas_call(functools.partial(layer_kernel, cfg), out_shape=pltpu.VMEM...]
where the time goes in v3:
time: 101 us
  Pallas kernels  98.8 us (98%)
  local copies, waits for them, and re-layouts  2.36 us (2%)
    pallas_call x1, Pallas kernels, local_layer(): pl.pallas_call(functools.partial(layer_kernel, cfg), out_shape=pltpu.VMEM...  98.8 us
    unnamed x1, local copies, waits for them, and re-layouts  2.36 us

profile of v3, /device:TPU:21, one launch (start us, length us, event | category | flops | bytes accessed | tf_op | source)
XLA Modules:
  0.0 101.2 jit_solution(14070105819500072815)
XLA Ops:
  0.0 98.8 %shard_map.244 = bf16[1024,2560]{1,0:T(8,128)(2,1)S(1)} custom-call(bf16[1024,2560]{1,0:T(8,128)(2,1)} %bitcast.43, s32[32]{0:T(128)} %ids_hbm.1, f32[20,128]{1,0:T(8,128)} %bitcast.61, f32[40,512]{1,0:T(8,128)} %constant.4.clone.cos_hbm, f32[40,512]{1,0:T(8,128)} %constant.5.clone.sin_hbm, bf16[160,2560]{1,0:T(8,128)(2,1)} %bitcast.44, ...), custom_call_target="tpu_custom_call" | custom-call | tf_op jit(solution)/shard_map/pallas_call | solution.py:633
  98.8 2.4 %copy.28 = bf16[32,32,2560]{2,1,0:T(8,128)(2,1)} copy(bf16[32,32,2560]{2,1,0:T(8,128)(2,1)S(1)} %bitcast.42) | data formatting | bytes 10485760

commit v4 on v3

--- a/solution.py
+++ b/solution.py
@@ -438,6 +438,22 @@
     def y_arrived(p):
         drain_recv(drecv.at[p], ad_r.at[p])
 
+    def ring_step(p, s):
+        for u in range(SUBS):
+            for way in range(2):
+                if s < hch - way:
+                    ring_part(p, way, s, u)
+
+    def ag_step(p, s):
+        for u in range(SUBS):
+            for way in range(2):
+                if s < hch - way:
+                    ag_part(p, way, s, u)
+
+    def finish_y(p):
+        for u in range(SUBS):
+            finish_part(p, u)
+
     w1_ld.wait()
     base_qkv(0)
     bt_ld.wait()
@@ -445,92 +461,50 @@
     bt_d2d.start()
     w2_ld.wait()
     base_gu(0)
-    bt_out(1).start()
     base_qkv(1)
     mid_forward()
     mid_service(1, 0)
+    bt_out(1).start()
     for cp in [cos_ld, sin_ld] + late:
         cp.wait()
     attend(0)
     gated(0)
+    mid_service(1, 1)
     groups(0, 0, 2)
-    mid_service(1, 1)
+    groups(0, 2, 4)
+    mid_service(1, 2)
+    ring_step(0, 0)
     mid_scatter(0)
+    base_gu(1)
+    mid_service(1, 3)
     bt_forward()
-    groups(0, 2, 4)
-    ring_part(0, 0, 0, 0)
-    ring_part(0, 1, 0, 0)
-    ring_part(0, 0, 0, 1)
-    ring_part(0, 1, 0, 1)
-    base_gu(1)
-    mid_service(1, 2)
-    ring_part(0, 1, 1, 0)
-    ring_part(0, 0, 1, 0)
-    ring_part(0, 1, 1, 1)
+    attend(1)
+    ring_step(0, 1)
+    gated(1)
     mid_gather(0)
-    ring_part(0, 0, 1, 1)
-    mid_service(1, 3)
-    attend(1)
-    ring_part(0, 0, 2, 0)
-    ring_part(0, 1, 2, 0)
-    gated(1)
+    groups(1, 0, 2)
+    ring_step(0, 2)
+    groups(1, 2, 4)
+    ring_step(1, 0)
     mid_scatter(1)
-    groups(1, 0, 2)
     bt_arrived()
+    ring_step(1, 1)
+    mid_gather(1)
     lora_out(0)
-    ring_part(0, 0, 2, 1)
-    ring_part(0, 1, 2, 1)
-    ring_part(0, 0, 3, 0)
-    groups(1, 2, 4)
-    ring_part(1, 0, 0, 1)
-    ring_part(1, 0, 0, 0)
-    ring_part(1, 1, 0, 0)
-    ring_part(1, 1, 0, 1)
-    ring_part(0, 0, 3, 1)
-    mid_gather(1)
-    finish_part(0, 0)
-    ring_part(1, 1, 1, 0)
-    ring_part(1, 0, 1, 1)
-    ring_part(1, 1, 1, 1)
-    ring_part(1, 0, 1, 0)
-    finish_part(0, 1)
-    ag_part(0, 1, 0, 0)
-    ring_part(1, 1, 2, 0)
-    ag_part(0, 0, 0, 0)
+    ring_step(0, 3)
+    ring_step(1, 2)
+    finish_y(0)
+    ring_step(1, 3)
+    ag_step(0, 0)
     lora_out(1)
-    ring_part(1, 1, 2, 1)
-    ring_part(1, 0, 2, 1)
-    ag_part(0, 1, 0, 1)
-    ring_part(1, 0, 2, 0)
-    ag_part(0, 1, 1, 0)
-    ag_part(0, 0, 0, 1)
-    ag_part(0, 0, 1, 0)
-    ring_part(1, 0, 3, 1)
-    ag_part(0, 1, 1, 1)
-    ring_part(1, 0, 3, 0)
-    ag_part(0, 1, 2, 0)
-    ag_part(0, 0, 1, 1)
-    ag_part(0, 0, 2, 0)
-    ag_part(0, 1, 2, 1)
-    finish_part(1, 1)
-    finish_part(1, 0)
-    ag_part(0, 0, 2, 1)
-    ag_part(0, 0, 3, 0)
-    ag_part(1, 1, 0, 1)
-    ag_part(1, 0, 0, 1)
-    ag_part(1, 1, 0, 0)
-    ag_part(1, 0, 0, 0)
-    ag_part(0, 0, 3, 1)
-    ag_part(1, 1, 1, 1)
-    ag_part(1, 0, 1, 1)
-    ag_part(1, 1, 1, 0)
-    ag_part(1, 0, 1, 0)
-    ag_part(1, 1, 2, 1)
-    ag_part(1, 0, 2, 1)
-    ag_part(1, 1, 2, 0)
-    ag_part(1, 0, 2, 0)
-    ag_part(1, 0, 3, 1)
-    ag_part(1, 0, 3, 0)
+    finish_y(1)
+    ag_step(0, 1)
+    ag_step(1, 0)
+    ag_step(0, 2)
+    ag_step(1, 1)
+    ag_step(0, 3)
+    ag_step(1, 2)
+    ag_step(1, 3)
     rank_sends_done()
     for p in range(PASSES):
         sum_sends_done(p)

time: 101 us -> 97.7 us (0.967)
  Pallas kernels: 98.8 us -> 95.2 us
    pallas_call x1, Pallas kernels: 98.8 us -> 95.2 us  [local_layer(): pl.pallas_call(functools.partial(layer_kernel, cfg), out_shape=pltpu.VMEM...]
where the time goes in v4:
time: 97.7 us; the launch traced here: 97.6 us
  Pallas kernels  95.2 us (97%)
  local copies, waits for them, and re-layouts  2.36 us (2%)
    pallas_call x1, Pallas kernels, local_layer(): pl.pallas_call(functools.partial(layer_kernel, cfg), out_shape=pltpu.VMEM...  95.2 us
    unnamed x1, local copies, waits for them, and re-layouts  2.36 us

profile of v4, /device:TPU:21, one launch (start us, length us, event | category | flops | bytes accessed | tf_op | source)
XLA Modules:
  0.0 97.6 jit_solution(4072385814059550014)
XLA Ops:
  0.0 95.2 %shard_map.244 = bf16[1024,2560]{1,0:T(8,128)(2,1)S(1)} custom-call(bf16[1024,2560]{1,0:T(8,128)(2,1)} %bitcast.43, s32[32]{0:T(128)} %ids_hbm.1, f32[20,128]{1,0:T(8,128)} %bitcast.61, f32[40,512]{1,0:T(8,128)} %constant.4.clone.cos_hbm, f32[40,512]{1,0:T(8,128)} %constant.5.clone.sin_hbm, bf16[160,2560]{1,0:T(8,128)(2,1)} %bitcast.44, ...), custom_call_target="tpu_custom_call" | custom-call | tf_op jit(solution)/shard_map/pallas_call | solution.py:607
  95.3 2.4 %copy.28 = bf16[32,32,2560]{2,1,0:T(8,128)(2,1)} copy(bf16[32,32,2560]{2,1,0:T(8,128)(2,1)S(1)} %bitcast.42) | data formatting | bytes 10485760

commit v5 on v4

--- a/solution.py
+++ b/solution.py
@@ -488,21 +488,21 @@
     ring_step(1, 0)
     mid_scatter(1)
     bt_arrived()
+    lora_out(0)
+    ring_step(0, 3)
     ring_step(1, 1)
     mid_gather(1)
-    lora_out(0)
-    ring_step(0, 3)
+    finish_y(0)
     ring_step(1, 2)
-    finish_y(0)
+    ag_step(0, 0)
     ring_step(1, 3)
-    ag_step(0, 0)
     lora_out(1)
+    ag_step(0, 1)
     finish_y(1)
-    ag_step(0, 1)
+    ag_step(0, 2)
     ag_step(1, 0)
-    ag_step(0, 2)
+    ag_step(0, 3)
     ag_step(1, 1)
-    ag_step(0, 3)
     ag_step(1, 2)
     ag_step(1, 3)
     rank_sends_done()

time: 97.7 us -> 98.8 us (1.011)
  Pallas kernels: 95.2 us -> 96.4 us
    pallas_call x1, Pallas kernels: 95.2 us -> 96.4 us  [local_layer(): pl.pallas_call(functools.partial(layer_kernel, cfg), out_shape=pltpu.VMEM...]
where the time goes in v5:
time: 98.8 us; the launch traced here: 98.7 us
  Pallas kernels  96.4 us (98%)
  local copies, waits for them, and re-layouts  2.36 us (2%)
    pallas_call x1, Pallas kernels, local_layer(): pl.pallas_call(functools.partial(layer_kernel, cfg), out_shape=pltpu.VMEM...  96.4 us
    unnamed x1, local copies, waits for them, and re-layouts  2.36 us

profile of v5, /device:TPU:21, one launch (start us, length us, event | category | flops | bytes accessed | tf_op | source)
XLA Modules:
  0.0 98.7 jit_solution(2796739862623099275)
XLA Ops:
  0.0 96.4 %shard_map.244 = bf16[1024,2560]{1,0:T(8,128)(2,1)S(1)} custom-call(bf16[1024,2560]{1,0:T(8,128)(2,1)} %bitcast.43, s32[32]{0:T(128)} %ids_hbm.1, f32[20,128]{1,0:T(8,128)} %bitcast.61, f32[40,512]{1,0:T(8,128)} %constant.4.clone.cos_hbm, f32[40,512]{1,0:T(8,128)} %constant.5.clone.sin_hbm, bf16[160,2560]{1,0:T(8,128)(2,1)} %bitcast.44, ...), custom_call_target="tpu_custom_call" | custom-call | tf_op jit(solution)/shard_map/pallas_call | solution.py:607
  96.4 2.4 %copy.28 = bf16[32,32,2560]{2,1,0:T(8,128)(2,1)} copy(bf16[32,32,2560]{2,1,0:T(8,128)(2,1)S(1)} %bitcast.42) | data formatting | bytes 10485760
